TPU v7x, 256 devices: a whole 4x4x8 slice. The times are simulated.
256 devices in a mesh: lat: 4 (over y), lon: 64 (over x, z, core).
Axes of the slice: x: 4, y: 4, z: 8, core: 2. Of those that a mesh axis runs over, the one named last changes fastest.
Arguments:
- right_side: float32 [512, 8192], P('lat', 'lon'), may hold values from -8 to 8
- surface_term: float32 [512, 8192], P('lat', 'lon'), may hold values from 0.0002 to 0.002
- east_coupling: float32 [512, 8192], P('lat', 'lon'), may hold values from 0.3 to 3
- north_coupling: float32 [512, 8192], P('lat', 'lon'), may hold values from 0.3 to 3
- neast_coupling: float32 [512, 8192], P('lat', 'lon'), may hold values from 0.1 to 0.5
- nwest_coupling: float32 [512, 8192], P('lat', 'lon'), may hold values from 0.1 to 0.5
- land_sea: int32 [512, 8192], P('lat', 'lon'), may hold values from 0 to 1, as said below
- fold_map: int32 [8192], P('lon'), may hold values from 0 to 8191, as said below
Outputs:
- solution: float32 [512, 8192], P('lat', 'lon')
- residual: float32 [512, 8192], P('lat', 'lon')
Inputs may be any that keep to these rules, and one draw needn't show every extreme that they name: fold_map[j] = (c - j) mod 8192 for one odd c: an involution of the columns with no fixed point. land_sea is 0 or 1; land lies in bands of 8 columns, each over one range of rows.
All inputs are finite; a program needn't handle non-finite values.
Results may differ from a plain program's by a relative error of at most 0.0015.
Values sent between devices are 32-bit elements.
No kernel may reach another device: no remote copies, remote signals or barrier semaphores. Data moves between devices by JAX's collectives and lax.ppermute only.
A program may use at most 64 MiB of HBM per device.

v0:
```python
import functools

import jax
import jax.numpy as jnp
from jax import lax
from jax.experimental import pallas as pl
from jax.experimental.pallas import tpu as pltpu
from jax.sharding import Mesh
from jax.sharding import PartitionSpec as P

LON = ("x", "z", "core")
NLON = 8192
COLS = 128
OWN = 32
GHOST = 8
WIDE = OWN + 2 * GHOST
PAD = COLS + 2 * GHOST
STEPS = 64
HALF = 4
TOTAL = 2 * HALF
SCALE = 1.0e-4
F32 = jnp.float32
HIGHEST = lax.Precision.HIGHEST
E, W, N, S, NE, SW, NW, SE, DIAG = range(9)
MULT, IPIV, LOWER, UPPER = range(4)


SIDE = 72


def params(mib=24):
    return pltpu.CompilerParams(vmem_limit_bytes=mib * 1024 * 1024)


def two_sum(a, b):
    s = a + b
    bb = s - a
    return s, (a - (s - bb)) + (b - bb)


def split(a):
    t = a * 4097.0
    hi = t - (t - a)
    return hi, a - hi


def two_prod(a, b):
    p = a * b
    ah, al = split(a)
    bh, bl = split(b)
    return p, ((ah * bh - p) + ah * bl + al * bh) + al * bl


def renorm(s, e):
    hi = s + e
    return hi, e - (hi - s)


def pair_sub(a, b):
    s, e = two_sum(a[0], -b[0])
    return renorm(s, e + (a[1] - b[1]))


def pair_mul(a, b):
    p, e = two_prod(a[0], b[0])
    return renorm(p, e + (a[0] * b[1] + a[1] * b[0]))


def pair_div(a, b):
    first = a[0] / b[0]
    zero = jnp.zeros_like(first)
    rest = pair_sub(a, pair_mul((first, zero), b))
    return renorm(first, rest[0] / b[0])


def sum_rows(values):
    s = values[0:8]
    e = jnp.zeros_like(s)
    for start in range(8, values.shape[0], 8):
        s, err = two_sum(s, values[start : start + 8])
        e = e + err
    for shift in (4, 2, 1):
        s_other = pltpu.roll(s, shift, 0)
        e_other = pltpu.roll(e, shift, 0)
        s, err = two_sum(s, s_other)
        e = e + e_other + err
    hi, lo = renorm(s, e)
    return hi[0:1], lo[0:1]


def small_solve(hi_row, lo_row, order):
    row = lax.broadcasted_iota(jnp.int32, (8, 128), 0)
    lane = lax.broadcasted_iota(jnp.int32, (8, 128), 1)

    def matrix(values):
        wide = jnp.broadcast_to(values, (8, 128))
        out = jnp.zeros((8, 128), F32)
        for i in range(order):
            turned = wide if i == 0 else pltpu.roll(wide, 128 - 16 * i, 1)
            out = jnp.where(row == i, turned, out)
        return jnp.where(lane < 16, out, 0.0)

    hi, lo = matrix(hi_row), matrix(lo_row)
    ratio = hi[3:4, 3:4] / hi[3:4, 2:3]
    start = jnp.sum(jnp.where(row == lane, hi, 0.0), axis=1, keepdims=True)
    live = jnp.ones((8, 128), F32)
    for k in range(order):
        col = tuple(jnp.broadcast_to(v[:, k : k + 1], (8, 128)) for v in (hi, lo))
        piv_row = tuple(jnp.broadcast_to(v[k : k + 1, :], (8, 128)) for v in (hi, lo))
        piv = tuple(jnp.broadcast_to(v[k : k + 1, k : k + 1], (8, 128)) for v in (hi, lo))
        good = piv[0] > 1e-11 * jnp.broadcast_to(start[k : k + 1, :], (8, 128))
        piv = (jnp.where(good, piv[0], 1.0), jnp.where(good, piv[1], 0.0))
        factor = pair_div(col, piv)
        new = pair_sub((hi, lo), pair_mul(factor, piv_row))
        change = good & (row != k)
        hi = jnp.where(change, new[0], hi)
        lo = jnp.where(change, new[1], lo)
        live = jnp.where((row == k) & ~good, 0.0, live)
    diag = jnp.sum(jnp.where(row == lane, hi, 0.0), axis=1, keepdims=True)
    diag = jnp.where((diag != 0.0) & (live[:, 0:1] > 0.0), diag, 1.0)
    y = jnp.broadcast_to(hi[:, 8:9] / diag, (8, 128)) * live
    y = jnp.where(row < order, y, 0.0)
    return y, jnp.broadcast_to(ratio, (8, 128))


def pack_body(place, rhs, surface, east, north, neast, nwest, land, out, *chunks):
    for k, ref in enumerate((rhs, surface, east, north, neast, nwest)):
        out[k] = ref[...].T
    out[6] = land[...].astype(F32).T
    for step, chunk in enumerate(chunks):
        start = pl.multiple_of(OWN * ((place[0] + step) & 3), OWN)
        chunk[...] = out[:, pl.ds(start, OWN), :]


def select_body(shift, low, main, high, out):
    i = lax.broadcasted_iota(jnp.int32, (PAD, COLS + 2 * SIDE), 0)
    u = lax.broadcasted_iota(jnp.int32, (PAD, COLS + 2 * SIDE), 1)
    reach = shift[0] + GHOST + SIDE
    plain = jnp.where(u == reach - i, 1.0, 0.0)
    moved = jnp.where(u == reach - 1 - i, 1.0, 0.0)
    for place, source in enumerate((0, 1, 2, 3, 5, 4, 6)):
        both = jnp.concatenate([low[source], main[source], high[source]], axis=0)
        facing = jnp.dot(moved if source == 2 else plain, both, precision=HIGHEST, preferred_element_type=F32)
        for part in range(4):
            out[part, place] = facing[OWN * part : OWN * part + WIDE, :]


def east_of(v):
    return pltpu.roll(v, 127, v.ndim - 1)


def west_of(v):
    return pltpu.roll(v, 1, v.ndim - 1)


def facing_of(v):
    return pltpu.roll(v, 64, v.ndim - 1)


def row_before(v):
    s = lax.broadcasted_iota(jnp.int32, (8, 128), 0)
    return jnp.where(s == 0, 0.0, pltpu.roll(v, 1, 0))


def row_after(v):
    s = lax.broadcasted_iota(jnp.int32, (8, 128), 0)
    return jnp.where(s == 7, 0.0, pltpu.roll(v, 7, 0))


def line_solve(load, lines, below_mat, above_mat, y_buf, g_buf, finish):
    zero = jnp.zeros((8, 128), F32)

    def forward(t, y):
        y = load(t) + lines[MULT, t] * y
        y_buf[t] = y
        return y

    lax.fori_loop(0, STEPS, forward, zero, unroll=8)

    def backward(k, x):
        t = STEPS - 1 - k
        x = y_buf[t] * lines[IPIV, t] + lines[MULT, t + 1] * x
        g_buf[t] = x
        return x

    lax.fori_loop(0, STEPS, backward, zero, unroll=8)
    first, last = g_buf[0], g_buf[STEPS - 1]
    below, above = zero, zero
    for k in range(8):
        for base, ends in ((0, first), (8, last)):
            end = jnp.broadcast_to(ends[k : k + 1, :], (8, 128))
            below = below + below_mat[base + k] * end
            above = above + above_mat[base + k] * end

    def combine(c, _):
        t0 = c * 8
        g = g_buf[pl.ds(t0, 8)] + lines[LOWER, pl.ds(t0, 8)] * below + lines[UPPER, pl.ds(t0, 8)] * above
        finish(t0, g)
        return 0

    lax.fori_loop(0, STEPS // 8, combine, 0, unroll=2)


def operate(v_ref, place, w_ref, coef, fold, vp, ve, vw):
    for t, v in ((0, row_before(v_ref[place, STEPS - 1])), (STEPS + 1, row_after(v_ref[place, 0]))):
        vp[t] = v
        ve[t] = east_of(v)
        vw[t] = west_of(v)

    def step(c, _):
        t = c * 4
        here, up, down = pl.ds(t + 1, 4), pl.ds(t + 2, 4), pl.ds(t, 4)
        at = pl.ds(t, 4)
        out = coef[DIAG, at] * vp[here]
        side = coef[E, at] * ve[here] + coef[W, at] * vw[here]
        north = coef[N, at] * vp[up] + coef[NE, at] * ve[up] + coef[NW, at] * vw[up]
        south = coef[S, at] * vp[down] + coef[SW, at] * vw[down] + coef[SE, at] * ve[down]
        w_ref[place, at] = out - (side + north + south)
        return 0

    lax.fori_loop(0, STEPS // 4, step, 0, unroll=2)
    w_ref[place, STEPS - 1] = w_ref[place, STEPS - 1] - fold[...] * facing_of(v_ref[place, STEPS - 1])


def store_field(v_ref, place, vp, ve, vw):
    def finish_with(value_of):
        def finish(t0, g):
            v = value_of(t0, g)
            v_ref[place, pl.ds(t0, 8)] = v
            vp[pl.ds(t0 + 1, 8)] = v
            ve[pl.ds(t0 + 1, 8)] = east_of(v)
            vw[pl.ds(t0 + 1, 8)] = west_of(v)

        return finish

    return finish_with


def gram_row(lefts, rights, pairs, exact, highs, lows, out):
    highs[...] = jnp.zeros(highs.shape, F32)
    lows[...] = jnp.zeros(lows.shape, F32)
    start = 0
    while start < len(pairs):
        end = start
        while end < len(pairs) and (pairs[end][0] == pairs[start][0] or end - start < 12) and end - start < 17:
            end += 1
        part = pairs[start:end]
        start = end

        def add(t, sums, part=part):
            left = {i: lefts[i](t) for i in sorted({i for i, _, _ in part})}
            right = {j: rights[j](t) for j in sorted({j for _, j, _ in part})}
            if not exact:
                return tuple((s + left[i] * right[j], e) for (s, e), (i, j, _) in zip(sums, part))
            left_halves = {i: split(v) for i, v in left.items()}
            right_halves = {j: split(v) for j, v in right.items()}
            out = []
            for (s, e), (i, j, _) in zip(sums, part):
                ah, al = left_halves[i]
                bh, bl = right_halves[j]
                s, err = two_sum(s, ah * bh)
                out.append((s, e + (err + (ah * bl + al * right[j]))))
            return tuple(out)

        zero = jnp.zeros((8, 128), F32)
        sums = lax.fori_loop(0, STEPS, add, tuple((zero, zero) for _ in part), unroll=1 if exact else 2)
        for (s, e), (_, _, lanes) in zip(sums, part):
            for lane in lanes:
                highs[pl.ds(lane, 8, stride=128), :] = s
                lows[pl.ds(lane, 8, stride=128), :] = e
    s, e = highs[0:128], lows[0:128]
    for k in range(1, 8):
        s, err = two_sum(s, highs[128 * k : 128 * k + 128])
        e = e + (err + lows[128 * k : 128 * k + 128])
    s, e = s.T, e.T
    hi, lo = sum_rows(jnp.concatenate([s[GHOST : GHOST + OWN], e[GHOST : GHOST + OWN]], axis=0))
    row = lax.broadcasted_iota(jnp.int32, (8, 128), 0)
    both = jnp.where((row & 1) == 0, jnp.broadcast_to(hi, (8, 128)), jnp.broadcast_to(lo, (8, 128)))
    out[...] = jnp.concatenate([both] * (out.shape[0] // 8), axis=0)


def gram_pairs(count):
    out = []
    for i in range(count):
        out += [(i, j, sorted({16 * i + j, 16 * j + i})) for j in range(i, count)]
        out.append((i, count, [16 * i + 8]))
    return out


def at(ref, *index):
    return lambda t: ref[(*index, t)]


def first_body(lat, c0, c1, c2, c3, lefts, rights, facing, coef, lines, below_mat, above_mat, fold, r0, v_ref, w_ref, gram, raw, grid, y_buf, g_buf, vp, ve, vw, highs, lows):
    s_id = lax.broadcasted_iota(jnp.int32, (8, 128), 0)
    zero = jnp.zeros((8, 128), F32)
    gap = jnp.zeros((64 - WIDE, 128), F32)
    for place in range(7):
        for step, chunk in enumerate((c0, c1, c2, c3)):
            source = (lat[0] - step) & 3
            left, right = lefts[(step - 1) % 4, place], rights[(step + 1) % 4, place]
            full = jnp.concatenate([left, chunk[place], right, gap, facing[source, place], gap], axis=0)
            raw[place, pl.ds(pl.multiple_of(128 * source, 128), 128), :] = full.T
        for t in range(STEPS):
            grid[place, t + 1] = raw[place, pl.ds(t, 8, stride=STEPS), :]
    top_north = grid[3, STEPS]
    top_ocean = grid[6, STEPS]
    last = s_id == 7
    fold_open = jnp.where(last, 0.5 * (top_north + facing_of(top_north)), 0.0)
    fold[...] = fold_open * top_ocean * facing_of(top_ocean)
    for place in (3, 4, 5):
        grid[place, STEPS] = jnp.where(last, 0.0, grid[place, STEPS])
    for place in (3, 4, 5, 6):
        grid[place, 0] = row_before(grid[place, STEPS])
        grid[place, STEPS + 1] = row_after(grid[place, 1])

    def weigh(t, _):
        o, o_up, o_down = grid[6, t + 1], grid[6, t + 2], grid[6, t]
        east = grid[2, t + 1]
        north, neast, nwest = grid[3, t + 1], grid[4, t + 1], grid[5, t + 1]
        south, s_neast, s_nwest = grid[3, t], grid[4, t], grid[5, t]
        open_sum = zero
        parts = (
            (E, east, east_of(o)),
            (W, west_of(east), west_of(o)),
            (N, north, o_up),
            (S, south, o_down),
            (NE, neast, east_of(o_up)),
            (SW, west_of(s_neast), west_of(o_down)),
            (NW, nwest, west_of(o_up)),
            (SE, east_of(s_nwest), east_of(o_down)),
        )
        for place, edge, other in parts:
            coef[place, t] = edge * o * other
            open_sum = open_sum + edge
        surface = grid[1, t + 1]
        coef[DIAG, t] = o * (surface + open_sum) + (1.0 - o)
        r0[t] = o * grid[0, t + 1]
        vw[t] = o * (surface + coef[N, t] + coef[S, t]) + (1.0 - o)
        return 0

    lax.fori_loop(0, STEPS, weigh, 0, unroll=2)
    surface = grid[1, STEPS]
    o = top_ocean
    coef[DIAG, STEPS - 1] = coef[DIAG, STEPS - 1] + o * fold_open

    def eliminate(t, carry):
        ratio, beyond = carry
        north = coef[N, t]
        pivot = vw[t] - coef[S, t] * ratio
        more, err = two_sum(pivot, -north)
        more = more + err
        y_buf[t] = more - ratio * beyond
        guess = north / pivot
        prod, err = two_prod(guess, pivot)
        return guess + ((north - prod) - err) / pivot, more

    ends = lax.fori_loop(0, STEPS, eliminate, (zero, zero), unroll=2)
    lax.fori_loop(0, STEPS, eliminate, tuple(row_before(v) for v in ends), unroll=2)

    def pivots(t, carry):
        before, beyond, response, source = carry
        rest = y_buf[t]
        mult = jnp.where(t == 0, zero, coef[S, t] * before)
        beyond = rest + jnp.where(t == 0, coef[S, 0], mult * beyond)
        inverse = 1.0 / (coef[N, t] + beyond)
        lines[MULT, t] = mult
        lines[IPIV, t] = inverse
        response = jnp.where(t == 0, coef[S, 0], mult * response)
        source = rest + mult * source
        g_buf[t] = response
        vp[t] = source
        return inverse, beyond, response, source

    lax.fori_loop(0, STEPS, pivots, (zero,) * 4, unroll=4)
    for t in range(STEPS, lines.shape[1]):
        lines[MULT, t] = zero

    def respond(k, carry):
        low, up, source = carry
        t = STEPS - 1 - k
        factor = lines[MULT, t + 1]
        inverse = lines[IPIV, t]
        low = g_buf[t] * inverse + factor * low
        up = jnp.where(k == 0, coef[N, STEPS - 1] * inverse, factor * up)
        source = vp[t] * inverse + factor * source
        lines[LOWER, t] = low
        lines[UPPER, t] = up
        ve[t] = source
        return low, up, source

    lax.fori_loop(0, STEPS, respond, (zero,) * 3, unroll=4)
    unit = lax.broadcasted_iota(jnp.int32, (16, 128), 0)
    low_first, low_last = lines[LOWER, 0], lines[LOWER, STEPS - 1]
    up_first, up_last = lines[UPPER, 0], lines[UPPER, STEPS - 1]

    def spread(v, s):
        return jnp.broadcast_to(v[s : s + 1, :], (16, 128))

    source_first, source_last = ve[0], ve[STEPS - 1]
    alphas, betas, dens = [jnp.zeros((16, 128), F32)], [jnp.zeros((16, 128), F32)], []
    short = jnp.ones((16, 128), F32)
    for s in range(8):
        alpha, beta = alphas[-1], betas[-1]
        g_first = jnp.where(unit == s, 1.0, 0.0)
        g_last = jnp.where(unit == 8 + s, 1.0, 0.0)
        lf, ll, uf, ul = (spread(v, s) for v in (low_first, low_last, up_first, up_last))
        sf, sl = spread(source_first, s), spread(source_last, s)
        den = 1.0 / (sf + uf + short * lf)
        dens.append(den)
        alphas.append(g_last + ll * (alpha + beta * den * (g_first + lf * alpha)))
        betas.append(ul + ll * beta * den * uf)
        short = sl + ll * (short + beta * den * (sf + lf * short))
    above = jnp.zeros((16, 128), F32)
    for s in range(7, -1, -1):
        alpha, beta = alphas[s], betas[s]
        above_mat[:, s, :] = above
        lf, uf = spread(low_first, s), spread(up_first, s)
        g_first = jnp.where(unit == s, 1.0, 0.0)
        above = dens[s] * (g_first + lf * alpha + uf * above)
        below_mat[:, s, :] = alpha + beta * above
    finish_with = functools.partial(store_field, v_ref)
    for i in range(HALF):
        load = (lambda t: r0[t]) if i == 0 else (lambda t, i=i: w_ref[i - 1, t])
        value = (lambda t0, g: g) if i == 0 else (lambda t0, g: g * SCALE)
        line_solve(load, lines, below_mat, above_mat, y_buf, g_buf, finish_with(i, vp, ve, vw)(value))
        operate(v_ref, i, w_ref, coef, fold, vp, ve, vw)
    lefts = [at(v_ref, i) for i in range(HALF)]
    rights = [at(w_ref, j) for j in range(HALF)] + [at(r0)]
    gram_row(lefts, rights, gram_pairs(HALF), False, highs, lows, gram)


def second_body(sums, coef, lines, below_mat, above_mat, fold, r0, v1, w1, r_ref, y_out, v_ref, w_ref, gram, y_buf, g_buf, vp, ve, vw, highs, lows):
    y, ratio = small_solve(*sum_rows(sums[...]), HALF)
    y_out[...] = y
    bound = ratio * (2.0 / SCALE)
    step = 2.0 / bound
    weights = [jnp.broadcast_to(y[i : i + 1, :], (8, 128)) for i in range(HALF)]

    def renew(t, _):
        r = r0[t]
        for i in range(HALF):
            r = r - weights[i] * w1[i, t]
        r_ref[t] = r
        return 0

    lax.fori_loop(0, STEPS, renew, 0, unroll=4)
    finish_with = functools.partial(store_field, v_ref)
    for i in range(HALF):
        load = (lambda t: r_ref[t]) if i == 0 else (lambda t, i=i: w_ref[i - 1, t])
        if i == 0:
            value = lambda t0, g: g
        elif i == 1:
            value = lambda t0, g: v_ref[0, pl.ds(t0, 8)] - step * g
        else:
            value = lambda t0, g, i=i: 2.0 * (v_ref[i - 1, pl.ds(t0, 8)] - step * g) - v_ref[i - 2, pl.ds(t0, 8)]
        line_solve(load, lines, below_mat, above_mat, y_buf, g_buf, finish_with(i, vp, ve, vw)(value))
        operate(v_ref, i, w_ref, coef, fold, vp, ve, vw)
    lefts = [at(ref, i) for ref in (v1, v_ref) for i in range(HALF)]
    rights = [at(ref, j) for ref in (w1, w_ref) for j in range(HALF)] + [at(r_ref)]
    gram_row(lefts, rights, gram_pairs(TOTAL), True, highs, lows, gram)


def last_body(sums, y1, r_ref, v1, w1, v2, w2, out, x_rows, r_rows):
    y, _ = small_solve(*sum_rows(sums[...]), TOTAL)
    w_weights = [jnp.broadcast_to(y[i : i + 1, :], (8, 128)) for i in range(TOTAL)]
    v_weights = [w + (y1[i : i + 1, :] if i < HALF else 0.0) for i, w in enumerate(w_weights)]
    for t in range(STEPS):
        x = jnp.zeros((8, 128), F32)
        r = r_ref[t]
        for i in range(HALF):
            x = x + v_weights[i] * v1[i, t]
            r = r - w_weights[i] * w1[i, t]
        for i in range(HALF):
            x = x + v_weights[HALF + i] * v2[i, t]
            r = r - w_weights[HALF + i] * w2[i, t]
        x_rows[pl.ds(t, 8, stride=STEPS), :] = x
        r_rows[pl.ds(t, 8, stride=STEPS), :] = r
    for place, rows in enumerate((x_rows, r_rows)):
        for part in range(4):
            out[part, place] = rows[128 * part : 128 * part + 128, :].T[GHOST : GHOST + OWN, :]


def unpack_body(recv, x, r):
    for place, ref in enumerate((x, r)):
        ref[...] = jnp.concatenate([recv[part, place] for part in range(4)], axis=0).T


def shape(*dims):
    return jax.ShapeDtypeStruct(dims, F32)


def vmem(*dims):
    return pltpu.VMEM(dims, F32)


FIELD = (STEPS, 8, 128)
SCRATCH = [vmem(*FIELD), vmem(*FIELD), vmem(STEPS + 2, 8, 128), vmem(STEPS + 2, 8, 128), vmem(STEPS + 2, 8, 128), vmem(1024, 128), vmem(1024, 128)]


def all_sums(gram):
    return lax.all_to_all(gram, ("lat", *LON), split_axis=0, concat_axis=0, tiled=True)


def ring(block, step):
    return lax.ppermute(block, LON, [(d, (d + step) % 64) for d in range(64)])


def reflect(block, half):
    def branch(q):
        return lambda b: lax.ppermute(b, LON, [(d, (2 * q - d) % 64) for d in range(64)])

    return lax.switch(half, [branch(q) for q in range(32)], block)


def strips(block, odd):
    def even_branch(b):
        return ring(b[:, COLS - SIDE :], -1), b, ring(b[:, :SIDE], 1)

    def odd_branch(b):
        return b[:, COLS - SIDE :], ring(b, 1), ring(b[:, :SIDE], 2)

    return lax.cond(odd == 0, even_branch, odd_branch, block)


def shards(right_side, surface_term, east, north, neast, nwest, land_sea, fold_map):
    lat = lax.axis_index("lat").reshape(1)
    offset = (fold_map[0] + COLS * lax.axis_index(LON)) % NLON
    centre = ((offset - COLS // 2) % NLON) // COLS
    shift = (offset - COLS // 2) % COLS + COLS // 2
    smem = pl.BlockSpec(memory_space=pltpu.SMEM)
    whole = pl.BlockSpec(memory_space=pltpu.VMEM)
    packed, *chunks = pl.pallas_call(
        pack_body,
        in_specs=[smem] + [whole] * 7,
        out_shape=(shape(7, COLS, 128),) + (shape(7, OWN, 128),) * 4,
        name="pack",
    )(lat, right_side, surface_term, east, north, neast, nwest, land_sea)
    for step in range(1, 4):
        chunks[step] = lax.ppermute(chunks[step], "lat", [(i, (i + step) % 4) for i in range(4)])
    low, main, high = strips(reflect(packed, centre // 2), centre % 2)
    where = [64 * (k % 4) + k // 4 for k in range(256)]
    lefts = jnp.stack([c[:, OWN - GHOST :] for c in chunks])
    rights = jnp.stack([c[:, :GHOST] for c in chunks])
    lefts = lax.ppermute(lefts, ("lat", *LON), [(where[k], where[(k + 1) % 256]) for k in range(256)])
    rights = lax.ppermute(rights, ("lat", *LON), [(where[k], where[k - 1]) for k in range(256)])
    windows = pl.pallas_call(
        select_body,
        in_specs=[smem] + [whole] * 3,
        out_shape=shape(4, 7, WIDE, 128),
        name="select",
        compiler_params=params(),
    )(shift.reshape(1), low, main, high)
    facing = lax.all_to_all(windows, "lat", split_axis=0, concat_axis=0, tiled=True)
    coef, lines, below_mat, above_mat, fold, r0, v1, w1, gram = pl.pallas_call(
        first_body,
        out_shape=(
            shape(9, *FIELD),
            shape(4, STEPS + 8, 8, 128),
            shape(16, 8, 128),
            shape(16, 8, 128),
            shape(8, 128),
            shape(*FIELD),
            shape(HALF, *FIELD),
            shape(HALF, *FIELD),
            shape(512, 128),
        ),
        scratch_shapes=[vmem(7, 512, 128), vmem(7, STEPS + 2, 8, 128), *SCRATCH],
        in_specs=[smem] + [whole] * 7,
        name="phase_one",
        compiler_params=params(),
    )(lat, *chunks, lefts, rights, facing)
    sums = all_sums(gram)
    r4, y1, v2, w2, gram = pl.pallas_call(
        second_body,
        out_shape=(
            shape(*FIELD),
            shape(8, 128),
            shape(HALF, *FIELD),
            shape(HALF, *FIELD),
            shape(512, 128),
        ),
        scratch_shapes=SCRATCH,
        name="phase_two",
        compiler_params=params(),
    )(sums, coef, lines, below_mat, above_mat, fold, r0, v1, w1)
    sums = all_sums(gram)
    pieces = pl.pallas_call(
        last_body,
        out_shape=shape(4, 2, OWN, 128),
        scratch_shapes=[vmem(512, 128), vmem(512, 128)],
        name="combine",
        compiler_params=params(),
    )(sums, y1, r4, v1, w1, v2, w2)
    columns = lax.all_to_all(pieces, "lat", split_axis=0, concat_axis=0, tiled=True)
    return pl.pallas_call(unpack_body, out_shape=(shape(128, COLS), shape(128, COLS)), name="unpack")(columns)


def solution(mesh):
    finer = Mesh(mesh.devices.reshape(mesh.shape["lat"], 4, 8, 2), ("lat", *LON))
    field = P("lat", LON)
    return jax.shard_map(
        shards,
        mesh=finer,
        in_specs=(field,) * 7 + (P(LON),),
        out_specs=(field, field),
        check_vma=False,
    )
```

profile of v0, /device:TPU:1, one launch (start us, length us, event | category | flops | bytes accessed | tf_op | source)
XLA Modules:
  0.0 201.5 jit_solution(16679614163046942611)
XLA Ops:
  0.6 2.0 %pack.1 = (f32[7,128,128]{2,1,0:T(8,128)S(1)}, f32[7,32,128]{2,1,0:T(8,128)}, f32[7,32,128]{2,1,0:T(8,128)}, f32[7,32,128]{2,1,0:T(8,128)}, f32[7,32,128]{2,1,0:T(8,128)}) custom-call(s32[1]{0:T(128)} %bitcast.place.lat, f32[128,128]{1,0:T(8,128)} %rhs.1, f32[128,128]{1,0:T(8,128)} %surface.1, f32[128,128]{1,0:T(8,128)} %east.1, f32[128,128]{1,0:T(8,128)} %north.1, ...), custom_call_target="tpu_custom_call" | custom-call | tf_op jit(solution)/shard_map/pack/pallas_call | solution.py:533
  2.7 13.8 %collective-permute-start.36 = (f32[7,32,128]{2,1,0:T(8,128)}, f32[7,32,128]{2,1,0:T(8,128)S(1)}, u32[]{:S(2)}, u32[]{:S(2)}) collective-permute-start(f32[7,32,128]{2,1,0:T(8,128)} %get-tuple-element.92), channel_id=1, source_target_pairs={{0,64},{64,128},{128,192},{192,0},{1,65},{65,129},{129,193},{193,1... | collective-permute-start | bytes 344072 | tf_op jit(solution)/shard_map/ppermute | solution.py:540
  16.5 11.8 %collective-permute-start.37 = (f32[7,32,128]{2,1,0:T(8,128)}, f32[7,32,128]{2,1,0:T(8,128)S(1)}, u32[]{:S(2)}, u32[]{:S(2)}) collective-permute-start(f32[7,32,128]{2,1,0:T(8,128)} %get-tuple-element.93), channel_id=1, source_target_pairs={{0,128},{64,192},{128,0},{192,64},{1,129},{65,193},{129,1},{193,65... | collective-permute-start | bytes 344072 | tf_op jit(solution)/shard_map/ppermute | solution.py:540
  28.3 11.8 %collective-permute-start.38 = (f32[7,32,128]{2,1,0:T(8,128)}, f32[7,32,128]{2,1,0:T(8,128)S(1)}, u32[]{:S(2)}, u32[]{:S(2)}) collective-permute-start(f32[7,32,128]{2,1,0:T(8,128)} %get-tuple-element.94), channel_id=1, source_target_pairs={{0,192},{64,0},{128,64},{192,128},{1,193},{65,1},{129,65},{193,129... | collective-permute-start | bytes 344072 | tf_op jit(solution)/shard_map/ppermute | solution.py:540
  40.9 17.6 %conditional.2 = (f32[7,128,128]{2,1,0:T(8,128)}) conditional(s32[]{:T(128)} %clamp.3, f32[7,128,128]{2,1,0:T(8,128)S(1)} %get-tuple-element.95, f32[7,128,128]{2,1,0:T(8,128)S(1)} %get-tuple-element.95, f32[7,128,128]{2,1,0:T(8,128)S(1)} %get-tuple-element.95, f32[7,128,128]{2,1,0:T(8,128)S(1)} %get-tuple-element.95, ...), branch_computations={%region_0.1_spmd, %region_1.2_spmd, %region_2.3_spmd, %region_3.4_... | conditional | bytes 1835056 | solution.py:513
  40.9 6.6 %collective-permute-start.12 = (f32[7,128,128]{2,1,0:T(8,128)S(1)}, f32[7,128,128]{2,1,0:T(8,128)}, u32[]{:S(2)}, u32[]{:S(2)}) collective-permute-start(f32[7,128,128]{2,1,0:T(8,128)S(1)} %param.12), channel_id=1, source_target_pairs={{0,24},{1,23},{2,22},{3,21},{4,20},{5,19},{6,18},{7,17},{8,16},{9,... | collective-permute-start | bytes 1376264 | tf_op jit(solution)/shard_map/cond/branch_12_fun/ppermute | solution.py:511
  47.6 10.9 %collective-permute-done.12 = f32[7,128,128]{2,1,0:T(8,128)} collective-permute-done((f32[7,128,128]{2,1,0:T(8,128)S(1)}, f32[7,128,128]{2,1,0:T(8,128)}, u32[]{:S(2)}, u32[]{:S(2)}) %collective-permute-start.12) | collective-permute-done | bytes 458784 | tf_op jit(solution)/shard_map/cond/branch_12_fun/ppermute | solution.py:511
  58.4 16.0 %conditional.3 = (f32[7,72,128]{2,1,0:T(8,128)}, f32[7,128,128]{2,1,0:T(8,128)S(1)}, f32[7,72,128]{2,1,0:T(8,128)}) conditional(s32[]{:T(128)} %convert_element_type.3, f32[7,128,128]{2,1,0:T(8,128)} %get-tuple-element.131, f32[7,128,128]{2,1,0:T(8,128)} %get-tuple-element.131), branch_computations={%region_32.33_spmd, %region_33.34_spmd} | conditional | bytes 4014184 | solution.py:523
  58.4 1.1 fusion.1
  59.6 9.0 %collective-permute-start.35 = (f32[7,72,128]{2,1,0:T(8,128)S(1)}, f32[7,72,128]{2,1,0:T(8,128)}, u32[]{:S(2)}, u32[]{:S(2)}) collective-permute-start(f32[7,72,128]{2,1,0:T(8,128)S(1)} %get-tuple-element.115), channel_id=1, source_target_pairs={{0,1},{1,2},{2,3},{3,4},{4,5},{5,6},{6,7},{7,8},{8,9},{9,10},{10,1... | collective-permute-start | bytes 774152 | tf_op jit(solution)/shard_map/cond/branch_1_fun/ppermute | solution.py:506
  69.6 2.3 %collective-permute-done.35 = f32[7,72,128]{2,1,0:T(8,128)} collective-permute-done((f32[7,72,128]{2,1,0:T(8,128)S(1)}, f32[7,72,128]{2,1,0:T(8,128)}, u32[]{:S(2)}, u32[]{:S(2)}) %collective-permute-start.35) | collective-permute-done | bytes 258080 | tf_op jit(solution)/shard_map/cond/branch_1_fun/ppermute | solution.py:506
  71.9 2.6 %collective-permute-done.34 = f32[7,72,128]{2,1,0:T(8,128)} collective-permute-done((f32[7,72,128]{2,1,0:T(8,128)S(1)}, f32[7,72,128]{2,1,0:T(8,128)}, u32[]{:S(2)}, u32[]{:S(2)}) %collective-permute-start.34) | collective-permute-done | bytes 258080 | tf_op jit(solution)/shard_map/cond/branch_1_fun/ppermute | solution.py:506
  74.5 3.4 %select.17 = f32[4,7,48,128]{3,2,1,0:T(8,128)} custom-call(s32[1]{0:T(128)} %bitcast.10.shift, f32[7,72,128]{2,1,0:T(8,128)} %get-tuple-element.96.low, f32[7,128,128]{2,1,0:T(8,128)S(1)} %get-tuple-element.97.main, f32[7,72,128]{2,1,0:T(8,128)} %get-tuple-element.98.high), custom_call_target="tpu_custom_call" | custom-call | tf_op jit(solution)/shard_map/select/pallas_call | solution.py:547
  77.8 4.1 %all-to-all-start = ((f32[4,7,48,128]{3,2,1,0:T(8,128)}), f32[4,7,48,128]{3,2,1,0:T(8,128)S(1)}, u32[]{:S(2)}, u32[]{:S(2)}) async-start(f32[4,7,48,128]{3,2,1,0:T(8,128)} %select.17), calls=%async_computation | async-start | bytes 1376256 | tf_op jit(solution)/shard_map/all_to_all | solution.py:554
  82.0 11.9 %collective-permute-start.39 = (f32[4,7,8,128]{3,2,1,0:T(8,128)S(1)}, f32[4,7,8,128]{3,2,1,0:T(8,128)S(1)}, u32[]{:S(2)}, u32[]{:S(2)}) collective-permute-start(f32[4,7,8,128]{3,2,1,0:T(8,128)S(1)} %pad_maximum_fusion), channel_id=1, source_target_pairs={{0,64},{64,128},{128,192},{192,1},{1,65},{65,129},{129,193},{193,2... | collective-permute-start | bytes 344072 | tf_op jit(solution)/shard_map/ppermute | solution.py:545
  93.9 11.9 %collective-permute-start.40 = (f32[4,7,8,128]{3,2,1,0:T(8,128)S(1)}, f32[4,7,8,128]{3,2,1,0:T(8,128)S(1)}, u32[]{:S(2)}, u32[]{:S(2)}) collective-permute-start(f32[4,7,8,128]{3,2,1,0:T(8,128)S(1)} %pad_maximum_fusion.1), channel_id=1, source_target_pairs={{0,255},{64,0},{128,64},{192,128},{1,192},{65,1},{129,65},{193,129... | collective-permute-start | bytes 344072 | tf_op jit(solution)/shard_map/ppermute | solution.py:546
  105.9 4.5 %collective-permute-done.40.rights = f32[4,7,8,128]{3,2,1,0:T(8,128)S(1)} collective-permute-done((f32[4,7,8,128]{3,2,1,0:T(8,128)S(1)}, f32[4,7,8,128]{3,2,1,0:T(8,128)S(1)}, u32[]{:S(2)}, u32[]{:S(2)}) %collective-permute-start.40) | collective-permute-done | bytes 114720 | tf_op jit(solution)/shard_map/ppermute | solution.py:546
  110.3 14.2 %phase_one.1 = (f32[9,64,8,128]{3,2,1,0:T(8,128)S(1)}, f32[4,72,8,128]{3,2,1,0:T(8,128)S(1)}, f32[16,8,128]{2,1,0:T(8,128)S(1)}, f32[16,8,128]{2,1,0:T(8,128)S(1...) custom-call(s32[1]{0:T(128)} %bitcast.place.lat, ...), custom_call_target="tpu_custom_call" | custom-call | tf_op jit(solution)/shard_map/phase_one/pallas_call | solution.py:555
  124.5 29.6 %all_to_all.32 = f32[256,2,128]{2,1,0:T(2,128)S(1)} all-to-all(f32[256,2,128]{2,1,0:T(2,128)S(1)} %bitcast.26), channel_id=1, replica_groups=mesh['lat'=4,'x'=4,'z'=8,'core'=2] {'lat','x','z','core'}, dimensions={0} | all-to-all | bytes 524288 | tf_op jit(solution)/shard_map/all_to_all | solution.py:502
  154.1 14.5 %phase_two.1 = (f32[64,8,128]{2,1,0:T(8,128)S(1)}, f32[8,128]{1,0:T(8,128)S(1)}, f32[4,64,8,128]{3,2,1,0:T(8,128)S(1)}, f32[4,64,8,128]{3,2,1,0:T(8,128)S(1)}, f32[512,128]{1,0:T(8,128)S(1)}) custom-call(f32[512,128]{1,0:T(8,128)S(1)} %bitcast.25, f32[9,64,8,128]{3,2,1,0:T(8,128)S(1)} %get-tuple-element.100.coef, ...), custom_call_target="tpu_custom_call" | custom-call | tf_op jit(solution)/shard_map/phase_two/pallas_call | solution.py:574
  168.7 21.2 %all_to_all.33 = f32[256,2,128]{2,1,0:T(2,128)S(1)} all-to-all(f32[256,2,128]{2,1,0:T(2,128)S(1)} %bitcast.27), channel_id=1, replica_groups=mesh['lat'=4,'x'=4,'z'=8,'core'=2] {'lat','x','z','core'}, dimensions={0} | all-to-all | bytes 524288 | tf_op jit(solution)/shard_map/all_to_all | solution.py:502
  189.9 2.0 %combine.1 = f32[4,2,32,128]{3,2,1,0:T(8,128)S(1)} custom-call(f32[512,128]{1,0:T(8,128)S(1)} %bitcast.24, f32[8,128]{1,0:T(8,128)S(1)} %get-tuple-element.109.y1, f32[64,8,128]{2,1,0:T(8,128)S(1)} %get-tuple-element.110.r_ref, f32[4,64,8,128]{3,2,1,0:T(8,128)S(1)} %get-tuple-element.106.v1, f32[4,64,8,128]{3,2,1,0:T(8,128)S(1)} %get-tuple-element.107.w1, ...), custom_call_target="tpu_custom_call" | custom-call | tf_op jit(solution)/shard_map/combine/pallas_call | solution.py:588
  192.0 7.9 %all_to_all.34.recv = f32[4,2,32,128]{3,2,1,0:T(8,128)} all-to-all(f32[4,2,32,128]{3,2,1,0:T(8,128)S(1)} %combine.1), channel_id=1, replica_groups=mesh['lat'=4,'x'=4,'z'=8,'core'=2] {'lat'}, dimensions={0} | all-to-all | bytes 262144 | tf_op jit(solution)/shard_map/all_to_all | solution.py:595
  199.8 1.7 unpack.1
  (15 shorter events, 1.1 us)
Async XLA Ops:
  2.7 79.2 %collective-permute-start.36 = (f32[7,32,128]{2,1,0:T(8,128)}, f32[7,32,128]{2,1,0:T(8,128)S(1)}, u32[]{:S(2)}, u32[]{:S(2)}) collective-permute-start(f32[7,32,128]{2,1,0:T(8,128)} %get-tuple-element.92), channel_id=1, source_target_pairs={{0,64},{64,128},{128,192},{192,0},{1,65},{65,129},{129,193},{193,1... | collective-permute-start | bytes 344072 | tf_op jit(solution)/shard_map/ppermute | solution.py:540
  16.5 65.5 %collective-permute-start.37 = (f32[7,32,128]{2,1,0:T(8,128)}, f32[7,32,128]{2,1,0:T(8,128)S(1)}, u32[]{:S(2)}, u32[]{:S(2)}) collective-permute-start(f32[7,32,128]{2,1,0:T(8,128)} %get-tuple-element.93), channel_id=1, source_target_pairs={{0,128},{64,192},{128,0},{192,64},{1,129},{65,193},{129,1},{193,65... | collective-permute-start | bytes 344072 | tf_op jit(solution)/shard_map/ppermute | solution.py:540
  28.3 53.7 %collective-permute-start.38 = (f32[7,32,128]{2,1,0:T(8,128)}, f32[7,32,128]{2,1,0:T(8,128)S(1)}, u32[]{:S(2)}, u32[]{:S(2)}) collective-permute-start(f32[7,32,128]{2,1,0:T(8,128)} %get-tuple-element.94), channel_id=1, source_target_pairs={{0,192},{64,0},{128,64},{192,128},{1,193},{65,1},{129,65},{193,129... | collective-permute-start | bytes 344072 | tf_op jit(solution)/shard_map/ppermute | solution.py:540
  40.9 17.5 %collective-permute-start.12 = (f32[7,128,128]{2,1,0:T(8,128)S(1)}, f32[7,128,128]{2,1,0:T(8,128)}, u32[]{:S(2)}, u32[]{:S(2)}) collective-permute-start(f32[7,128,128]{2,1,0:T(8,128)S(1)} %param.12), channel_id=1, source_target_pairs={{0,24},{1,23},{2,22},{3,21},{4,20},{5,19},{6,18},{7,17},{8,16},{9,... | collective-permute-start | bytes 1376264 | tf_op jit(solution)/shard_map/cond/branch_12_fun/ppermute | solution.py:511
  58.4 23.5 %copy-start = (f32[7,32,128]{2,1,0:T(8,128)S(1)}, f32[7,32,128]{2,1,0:T(8,128)}, u32[]{:S(2)}) copy-start(f32[7,32,128]{2,1,0:T(8,128)} %get-tuple-element.91.c0) | copy-start | bytes 344068
  59.6 12.3 %collective-permute-start.35 = (f32[7,72,128]{2,1,0:T(8,128)S(1)}, f32[7,72,128]{2,1,0:T(8,128)}, u32[]{:S(2)}, u32[]{:S(2)}) collective-permute-start(f32[7,72,128]{2,1,0:T(8,128)S(1)} %get-tuple-element.115), channel_id=1, source_target_pairs={{0,1},{1,2},{2,3},{3,4},{4,5},{5,6},{6,7},{7,8},{8,9},{9,10},{10,1... | collective-permute-start | bytes 774152 | tf_op jit(solution)/shard_map/cond/branch_1_fun/ppermute | solution.py:506
  68.6 5.9 %collective-permute-start.34 = (f32[7,72,128]{2,1,0:T(8,128)S(1)}, f32[7,72,128]{2,1,0:T(8,128)}, u32[]{:S(2)}, u32[]{:S(2)}) collective-permute-start(f32[7,72,128]{2,1,0:T(8,128)S(1)} %get-tuple-element.116), channel_id=1, source_target_pairs={{0,63},{1,0},{2,1},{3,2},{4,3},{5,4},{6,5},{7,6},{8,7},{9,8},{10,9... | collective-permute-start | bytes 774152 | tf_op jit(solution)/shard_map/cond/branch_1_fun/ppermute | solution.py:506
  77.8 32.5 %all-to-all-start = ((f32[4,7,48,128]{3,2,1,0:T(8,128)}), f32[4,7,48,128]{3,2,1,0:T(8,128)S(1)}, u32[]{:S(2)}, u32[]{:S(2)}) async-start(f32[4,7,48,128]{3,2,1,0:T(8,128)} %select.17), calls=%async_computation | async-start | bytes 1376256 | tf_op jit(solution)/shard_map/all_to_all | solution.py:554
  82.0 23.8 %collective-permute-start.39 = (f32[4,7,8,128]{3,2,1,0:T(8,128)S(1)}, f32[4,7,8,128]{3,2,1,0:T(8,128)S(1)}, u32[]{:S(2)}, u32[]{:S(2)}) collective-permute-start(f32[4,7,8,128]{3,2,1,0:T(8,128)S(1)} %pad_maximum_fusion), channel_id=1, source_target_pairs={{0,64},{64,128},{128,192},{192,1},{1,65},{65,129},{129,193},{193,2... | collective-permute-start | bytes 344072 | tf_op jit(solution)/shard_map/ppermute | solution.py:545
  93.9 16.4 %collective-permute-start.40 = (f32[4,7,8,128]{3,2,1,0:T(8,128)S(1)}, f32[4,7,8,128]{3,2,1,0:T(8,128)S(1)}, u32[]{:S(2)}, u32[]{:S(2)}) collective-permute-start(f32[4,7,8,128]{3,2,1,0:T(8,128)S(1)} %pad_maximum_fusion.1), channel_id=1, source_target_pairs={{0,255},{64,0},{128,64},{192,128},{1,192},{65,1},{129,65},{193,129... | collective-permute-start | bytes 344072 | tf_op jit(solution)/shard_map/ppermute | solution.py:546
where the time goes:
time: 203 us; the launch traced here: 202 us
  starting transfers between devices  81 us (40%)
  blocking collectives  58.7 us (29%)
  Pallas kernels  37.8 us (19%)
  waiting for transfers between devices  20.2 us (10%)
  local copies, waits for them, and re-layouts  2.19 us (1%)
    all_to_all x2, blocking collectives, all_sums(): lax.all_to_all(gram, ('lat', *LON), split_axis=0, concat_axis=0, tiled=True)  50.8 us
    ppermute x3, starting transfers between devices, shards(): lax.ppermute(chunks[step], 'lat', [(i, (i + step) % 4) for i in range(4)])  37.4 us
    pallas_call x1, Pallas kernels, shards(): pl.pallas_call(second_body, out_shape=(shape(*FIELD), shape(8, 128), shap...  14.5 us
    pallas_call x1, Pallas kernels, shards(): pl.pallas_call(first_body, out_shape=(shape(9, *FIELD), shape(4, STEPS +...  14.2 us
    ppermute x1, starting transfers between devices, shards(): lax.ppermute(rights, ('lat', *LON), [(where[k], where[k - 1]) for k in ra...  11.9 us
    ppermute x1, starting transfers between devices, shards(): lax.ppermute(lefts, ('lat', *LON), [(where[k], where[(k + 1) % 256]) for...  11.9 us
    ppermute x1, waiting for transfers between devices, branch(): lax.ppermute(b, LON, [(d, (2 * q - d) % 64) for d in range(64)])  10.9 us
    ppermute x2, starting transfers between devices, ring(): return lax.ppermute(block, LON, [(d, (d + step) % 64) for d in range(64)])  9.01 us
  transfers between devices with their start and end apart: 9, of which 4 were waited for; matrix products, arithmetic and copies ran while one was open for 1% of the time, Pallas kernels for 2%

commit v1 on v0

--- a/solution.py
+++ b/solution.py
@@ -506,21 +506,21 @@
     return lax.ppermute(block, LON, [(d, (d + step) % 64) for d in range(64)])
 
 
-def reflect(block, half):
+def reflect(block, quarter):
     def branch(q):
-        return lambda b: lax.ppermute(b, LON, [(d, (2 * q - d) % 64) for d in range(64)])
-
-    return lax.switch(half, [branch(q) for q in range(32)], block)
-
-
-def strips(block, odd):
-    def even_branch(b):
-        return ring(b[:, COLS - SIDE :], -1), b, ring(b[:, :SIDE], 1)
-
-    def odd_branch(b):
-        return b[:, COLS - SIDE :], ring(b, 1), ring(b[:, :SIDE], 2)
-
-    return lax.cond(odd == 0, even_branch, odd_branch, block)
+        return lambda b: lax.ppermute(b, LON, [(d, (4 * q - d) % 64) for d in range(64)])
+
+    return lax.switch(quarter, [branch(q) for q in range(16)], block)
+
+
+def strips(block, step):
+    def branch(p):
+        def moved(b, by):
+            return ring(b, by) if by else b
+
+        return lambda b: (moved(b[:, COLS - SIDE :], p - 1), moved(b, p), moved(b[:, :SIDE], p + 1))
+
+    return lax.switch(step, [branch(p) for p in (-1, 0, 1, 2)], block)
 
 
 def shards(right_side, surface_term, east, north, neast, nwest, land_sea, fold_map):
@@ -538,7 +538,8 @@
     )(lat, right_side, surface_term, east, north, neast, nwest, land_sea)
     for step in range(1, 4):
         chunks[step] = lax.ppermute(chunks[step], "lat", [(i, (i + step) % 4) for i in range(4)])
-    low, main, high = strips(reflect(packed, centre // 2), centre % 2)
+    ahead = (centre + 1) % 64
+    low, main, high = strips(reflect(packed, ahead // 4), ahead % 4)
     where = [64 * (k % 4) + k // 4 for k in range(256)]
     lefts = jnp.stack([c[:, OWN - GHOST :] for c in chunks])
     rights = jnp.stack([c[:, :GHOST] for c in chunks])

time: 203 us -> 159 us (0.78)
  starting transfers between devices: 81 us -> 23.4 us
  waiting for transfers between devices: 20.2 us -> 40.6 us
  blocking collectives: 58.7 us -> 54 us
    ppermute x3, starting transfers between devices: 37.4 us -> 6.06 us  [shards(): lax.ppermute(chunks[step], 'lat', [(i, (i + step) % 4) for i in range(4)])]
    ppermute x1, starting transfers between devices: 11.9 us -> 1.5 us  [shards(): lax.ppermute(lefts, ('lat', *LON), [(where[k], where[(k + 1) % 256]) for...]
    ppermute x1, waiting for transfers between devices: 0.01 us -> 10.4 us  [shards(): lax.ppermute(lefts, ('lat', *LON), [(where[k], where[(k + 1) % 256]) for...]
    ppermute x1, starting transfers between devices: 11.9 us -> 1.63 us  [shards(): lax.ppermute(rights, ('lat', *LON), [(where[k], where[k - 1]) for k in ra...]
    ppermute x1, waiting for transfers between devices: 10.9 us -> 20.2 us  [branch(): lax.ppermute(b, LON, [(d, (4 * q - d) % 64) for d in range(64)])]
    ppermute x2, starting transfers between devices: 9.01 us -> 2.3 us  [ring(): return lax.ppermute(block, LON, [(d, (d + step) % 64) for d in range(64)])]
    ppermute x2, waiting for transfers between devices: 4.84 us -> 10 us  [ring(): return lax.ppermute(block, LON, [(d, (d + step) % 64) for d in range(64)])]
    all_to_all x2, blocking collectives: 50.8 us -> 46.2 us  [all_sums(): lax.all_to_all(gram, ('lat', *LON), split_axis=0, concat_axis=0, tiled=True)]
  transfers between devices with their start and end apart: 9 -> 9, of which waited for: 4 -> 3; matrix products, arithmetic and copies ran while one was open for 1% -> 1% of each run, Pallas kernels for 2% -> 2%
where the time goes in v1:
time: 159 us
  blocking collectives  54 us (34%)
  waiting for transfers between devices  40.6 us (26%)
  Pallas kernels  38 us (24%)
  starting transfers between devices  23.4 us (15%)
  local copies, waits for them, and re-layouts  1.85 us (1%)
    all_to_all x2, blocking collectives, all_sums(): lax.all_to_all(gram, ('lat', *LON), split_axis=0, concat_axis=0, tiled=True)  46.2 us
    ppermute x1, waiting for transfers between devices, branch(): lax.ppermute(b, LON, [(d, (4 * q - d) % 64) for d in range(64)])  20.2 us
    pallas_call x1, Pallas kernels, shards(): pl.pallas_call(second_body, out_shape=(shape(*FIELD), shape(8, 128), shap...  14.5 us
    pallas_call x1, Pallas kernels, shards(): pl.pallas_call(first_body, out_shape=(shape(9, *FIELD), shape(4, STEPS +...  14.2 us
    ppermute x1, waiting for transfers between devices, shards(): lax.ppermute(lefts, ('lat', *LON), [(where[k], where[(k + 1) % 256]) for...  10.4 us
    ppermute x2, waiting for transfers between devices, ring(): return lax.ppermute(block, LON, [(d, (d + step) % 64) for d in range(64)])  10 us
    ppermute x1, starting transfers between devices, branch(): lax.ppermute(b, LON, [(d, (4 * q - d) % 64) for d in range(64)])  8.41 us
    all_to_all x1, blocking collectives, shards(): lax.all_to_all(pieces, 'lat', split_axis=0, concat_axis=0, tiled=True)  7.88 us
  transfers between devices with their start and end apart: 9, of which 3 were waited for; matrix products, arithmetic and copies ran while one was open for 1% of the time, Pallas kernels for 2%

profile of v1, /device:TPU:1, one launch (start us, length us, event | category | flops | bytes accessed | tf_op | source)
XLA Modules:
  0.0 159.4 jit_solution(715279604087141886)
XLA Ops:
  0.6 2.1 %pack.1 = (f32[7,128,128]{2,1,0:T(8,128)S(1)}, f32[7,32,128]{2,1,0:T(8,128)}, f32[7,32,128]{2,1,0:T(8,128)}, f32[7,32,128]{2,1,0:T(8,128)}, f32[7,32,128]{2,1,0:T(8,128)}) custom-call(s32[1]{0:T(128)} %bitcast.place.lat, f32[128,128]{1,0:T(8,128)} %rhs.1, f32[128,128]{1,0:T(8,128)} %surface.1, f32[128,128]{1,0:T(8,128)} %east.1, f32[128,128]{1,0:T(8,128)} %north.1, ...), custom_call_target="tpu_custom_call" | custom-call | tf_op jit(solution)/shard_map/pack/pallas_call | solution.py:533
  2.7 2.1 %collective-permute-start.25 = (f32[7,32,128]{2,1,0:T(8,128)}, f32[7,32,128]{2,1,0:T(8,128)S(1)}, u32[]{:S(2)}, u32[]{:S(2)}) collective-permute-start(f32[7,32,128]{2,1,0:T(8,128)} %get-tuple-element.62), channel_id=1, source_target_pairs={{0,64},{64,128},{128,192},{192,0},{1,65},{65,129},{129,193},{193,1... | collective-permute-start | bytes 344072 | tf_op jit(solution)/shard_map/ppermute | solution.py:540
  4.8 2.6 %collective-permute-start.26 = (f32[7,32,128]{2,1,0:T(8,128)}, f32[7,32,128]{2,1,0:T(8,128)S(1)}, u32[]{:S(2)}, u32[]{:S(2)}) collective-permute-start(f32[7,32,128]{2,1,0:T(8,128)} %get-tuple-element.63), channel_id=1, source_target_pairs={{0,128},{64,192},{128,0},{192,64},{1,129},{65,193},{129,1},{193,65... | collective-permute-start | bytes 344072 | tf_op jit(solution)/shard_map/ppermute | solution.py:540
  8.2 28.6 %conditional.2 = (f32[7,128,128]{2,1,0:T(8,128)}) conditional(s32[]{:T(128)} %clamp.7, f32[7,128,128]{2,1,0:T(8,128)S(1)} %get-tuple-element.65, f32[7,128,128]{2,1,0:T(8,128)S(1)} %get-tuple-element.65, f32[7,128,128]{2,1,0:T(8,128)S(1)} %get-tuple-element.65, f32[7,128,128]{2,1,0:T(8,128)S(1)} %get-tuple-element.65, ...), branch_computations={%region_0.1_spmd, %region_1.2_spmd, %region_2.3_spmd, %region_3.4_... | conditional | bytes 1835056 | solution.py:513
  8.2 8.4 %collective-permute-start.8 = (f32[7,128,128]{2,1,0:T(8,128)S(1)}, f32[7,128,128]{2,1,0:T(8,128)}, u32[]{:S(2)}, u32[]{:S(2)}) collective-permute-start(f32[7,128,128]{2,1,0:T(8,128)S(1)} %param.8), channel_id=1, source_target_pairs={{0,32},{1,31},{2,30},{3,29},{4,28},{5,27},{6,26},{7,25},{8,24},{9,... | collective-permute-start | bytes 1376264 | tf_op jit(solution)/shard_map/cond/branch_8_fun/ppermute | solution.py:511
  16.6 20.2 %collective-permute-done.8 = f32[7,128,128]{2,1,0:T(8,128)} collective-permute-done((f32[7,128,128]{2,1,0:T(8,128)S(1)}, f32[7,128,128]{2,1,0:T(8,128)}, u32[]{:S(2)}, u32[]{:S(2)}) %collective-permute-start.8) | collective-permute-done | bytes 458784 | tf_op jit(solution)/shard_map/cond/branch_8_fun/ppermute | solution.py:511
  36.8 14.2 %conditional.3 = (f32[7,72,128]{2,1,0:T(8,128)}, f32[7,128,128]{2,1,0:T(8,128)}, f32[7,72,128]{2,1,0:T(8,128)}) conditional(s32[]{:T(128)} %clamp.6, f32[7,128,128]{2,1,0:T(8,128)} %get-tuple-element.111, f32[7,128,128]{2,1,0:T(8,128)} %get-tuple-element.111, f32[7,128,128]{2,1,0:T(8,128)} %get-tuple-element.111, ...), branch_computations={%region_16.17_spmd, %region_17.18_spmd, %region_18.19_spmd, %regio... | conditional | bytes 4931728 | solution.py:523
  36.8 2.3 %collective-permute-start.20 = (f32[7,128,128]{2,1,0:T(8,128)}, f32[7,128,128]{2,1,0:T(8,128)}, u32[]{:S(2)}, u32[]{:S(2)}) collective-permute-start(f32[7,128,128]{2,1,0:T(8,128)} %param.18), channel_id=1, source_target_pairs={{0,1},{1,2},{2,3},{3,4},{4,5},{5,6},{6,7},{7,8},{8,9},{9,10},{10,1... | collective-permute-start | bytes 1376264 | tf_op jit(solution)/shard_map/cond/branch_2_fun/ppermute | solution.py:506
  39.1 1.8 %fusion.2 = (f32[7,72,128]{2,1,0:T(8,128)S(1)}, f32[7,72,128]{2,1,0:T(8,128)}) fusion(f32[7,128,128]{2,1,0:T(8,128)} %param.18), kind=kLoop, calls=%fused_computation.12 | loop fusion | bytes 1032192 | tf_op jit(solution)/shard_map/cond/branch_2_fun/slice | solution.py:521
  40.9 0.0 collective-permute-start.21
  40.9 10.0 %collective-permute-done.21 = f32[7,72,128]{2,1,0:T(8,128)} collective-permute-done((f32[7,72,128]{2,1,0:T(8,128)S(1)}, f32[7,72,128]{2,1,0:T(8,128)}, u32[]{:S(2)}, u32[]{:S(2)}) %collective-permute-start.21) | collective-permute-done | bytes 258080 | tf_op jit(solution)/shard_map/cond/branch_2_fun/ppermute | solution.py:506
  51.0 1.3 collective-permute-start.27
  52.3 3.5 %select.19 = f32[4,7,48,128]{3,2,1,0:T(8,128)} custom-call(s32[1]{0:T(128)} %bitcast.10.shift, f32[7,72,128]{2,1,0:T(8,128)} %get-tuple-element.66.low, f32[7,128,128]{2,1,0:T(8,128)} %get-tuple-element.67.main, f32[7,72,128]{2,1,0:T(8,128)} %get-tuple-element.68.high), custom_call_target="tpu_custom_call" | custom-call | tf_op jit(solution)/shard_map/select/pallas_call | solution.py:548
  55.8 3.5 %all-to-all-start = ((f32[4,7,48,128]{3,2,1,0:T(8,128)}), f32[4,7,48,128]{3,2,1,0:T(8,128)S(1)}, u32[]{:S(2)}, u32[]{:S(2)}) async-start(f32[4,7,48,128]{3,2,1,0:T(8,128)} %select.19), calls=%async_computation | async-start | bytes 1376256 | tf_op jit(solution)/shard_map/all_to_all | solution.py:555
  59.4 1.5 collective-permute-start.28
  60.9 1.6 %collective-permute-start.29 = (f32[4,7,8,128]{3,2,1,0:T(8,128)S(1)}, f32[4,7,8,128]{3,2,1,0:T(8,128)S(1)}, u32[]{:S(2)}, u32[]{:S(2)}) collective-permute-start(f32[4,7,8,128]{3,2,1,0:T(8,128)S(1)} %pad_maximum_fusion.1), channel_id=1, source_target_pairs={{0,255},{64,0},{128,64},{192,128},{1,192},{65,1},{129,65},{193,129... | collective-permute-start | bytes 344072 | tf_op jit(solution)/shard_map/ppermute | solution.py:547
  62.5 10.4 %collective-permute-done.28.lefts = f32[4,7,8,128]{3,2,1,0:T(8,128)S(1)} collective-permute-done((f32[4,7,8,128]{3,2,1,0:T(8,128)S(1)}, f32[4,7,8,128]{3,2,1,0:T(8,128)S(1)}, u32[]{:S(2)}, u32[]{:S(2)}) %collective-permute-start.28) | collective-permute-done | bytes 114720 | tf_op jit(solution)/shard_map/ppermute | solution.py:546
  72.9 14.2 %phase_one.1 = (f32[9,64,8,128]{3,2,1,0:T(8,128)S(1)}, f32[4,72,8,128]{3,2,1,0:T(8,128)S(1)}, f32[16,8,128]{2,1,0:T(8,128)S(1)}, f32[16,8,128]{2,1,0:T(8,128)S(1...) custom-call(s32[1]{0:T(128)} %bitcast.place.lat, ...), custom_call_target="tpu_custom_call" | custom-call | tf_op jit(solution)/shard_map/phase_one/pallas_call | solution.py:556
  87.1 24.9 %all_to_all.32 = f32[256,2,128]{2,1,0:T(2,128)S(1)} all-to-all(f32[256,2,128]{2,1,0:T(2,128)S(1)} %bitcast.26), channel_id=1, replica_groups=mesh['lat'=4,'x'=4,'z'=8,'core'=2] {'lat','x','z','core'}, dimensions={0} | all-to-all | bytes 524288 | tf_op jit(solution)/shard_map/all_to_all | solution.py:502
  112.0 14.5 %phase_two.1 = (f32[64,8,128]{2,1,0:T(8,128)S(1)}, f32[8,128]{1,0:T(8,128)S(1)}, f32[4,64,8,128]{3,2,1,0:T(8,128)S(1)}, f32[4,64,8,128]{3,2,1,0:T(8,128)S(1)}, f32[512,128]{1,0:T(8,128)S(1)}) custom-call(f32[512,128]{1,0:T(8,128)S(1)} %bitcast.25, f32[9,64,8,128]{3,2,1,0:T(8,128)S(1)} %get-tuple-element.70.coef, ...), custom_call_target="tpu_custom_call" | custom-call | tf_op jit(solution)/shard_map/phase_two/pallas_call | solution.py:575
  126.6 21.2 %all_to_all.33 = f32[256,2,128]{2,1,0:T(2,128)S(1)} all-to-all(f32[256,2,128]{2,1,0:T(2,128)S(1)} %bitcast.27), channel_id=1, replica_groups=mesh['lat'=4,'x'=4,'z'=8,'core'=2] {'lat','x','z','core'}, dimensions={0} | all-to-all | bytes 524288 | tf_op jit(solution)/shard_map/all_to_all | solution.py:502
  147.8 2.0 %combine.1 = f32[4,2,32,128]{3,2,1,0:T(8,128)S(1)} custom-call(f32[512,128]{1,0:T(8,128)S(1)} %bitcast.24, f32[8,128]{1,0:T(8,128)S(1)} %get-tuple-element.79.y1, f32[64,8,128]{2,1,0:T(8,128)S(1)} %get-tuple-element.80.r_ref, f32[4,64,8,128]{3,2,1,0:T(8,128)S(1)} %get-tuple-element.76.v1, f32[4,64,8,128]{3,2,1,0:T(8,128)S(1)} %get-tuple-element.77.w1, ...), custom_call_target="tpu_custom_call" | custom-call | tf_op jit(solution)/shard_map/combine/pallas_call | solution.py:589
  149.9 7.9 %all_to_all.34.recv = f32[4,2,32,128]{3,2,1,0:T(8,128)} all-to-all(f32[4,2,32,128]{3,2,1,0:T(8,128)S(1)} %combine.1), channel_id=1, replica_groups=mesh['lat'=4,'x'=4,'z'=8,'core'=2] {'lat'}, dimensions={0} | all-to-all | bytes 262144 | tf_op jit(solution)/shard_map/all_to_all | solution.py:596
  157.7 1.7 %unpack.1 = (f32[128,128]{1,0:T(8,128)}, f32[128,128]{1,0:T(8,128)}) custom-call(f32[4,2,32,128]{3,2,1,0:T(8,128)} %all_to_all.34.recv), custom_call_target="tpu_custom_call" | custom-call | tf_op jit(solution)/shard_map/unpack/pallas_call | solution.py:597
  (16 shorter events, 0.1 us)
Async XLA Ops:
  2.7 56.6 %collective-permute-start.25 = (f32[7,32,128]{2,1,0:T(8,128)}, f32[7,32,128]{2,1,0:T(8,128)S(1)}, u32[]{:S(2)}, u32[]{:S(2)}) collective-permute-start(f32[7,32,128]{2,1,0:T(8,128)} %get-tuple-element.62), channel_id=1, source_target_pairs={{0,64},{64,128},{128,192},{192,0},{1,65},{65,129},{129,193},{193,1... | collective-permute-start | bytes 344072 | tf_op jit(solution)/shard_map/ppermute | solution.py:540
  4.8 54.5 %collective-permute-start.26 = (f32[7,32,128]{2,1,0:T(8,128)}, f32[7,32,128]{2,1,0:T(8,128)S(1)}, u32[]{:S(2)}, u32[]{:S(2)}) collective-permute-start(f32[7,32,128]{2,1,0:T(8,128)} %get-tuple-element.63), channel_id=1, source_target_pairs={{0,128},{64,192},{128,0},{192,64},{1,129},{65,193},{129,1},{193,65... | collective-permute-start | bytes 344072 | tf_op jit(solution)/shard_map/ppermute | solution.py:540
  8.2 28.6 %collective-permute-start.8 = (f32[7,128,128]{2,1,0:T(8,128)S(1)}, f32[7,128,128]{2,1,0:T(8,128)}, u32[]{:S(2)}, u32[]{:S(2)}) collective-permute-start(f32[7,128,128]{2,1,0:T(8,128)S(1)} %param.8), channel_id=1, source_target_pairs={{0,32},{1,31},{2,30},{3,29},{4,28},{5,27},{6,26},{7,25},{8,24},{9,... | collective-permute-start | bytes 1376264 | tf_op jit(solution)/shard_map/cond/branch_8_fun/ppermute | solution.py:511
  36.8 14.2 %copy-start.1 = (f32[7,32,128]{2,1,0:T(8,128)S(1)}, f32[7,32,128]{2,1,0:T(8,128)}, u32[]{:S(2)}) copy-start(f32[7,32,128]{2,1,0:T(8,128)} %get-tuple-element.64) | copy-start | bytes 344068
  36.8 14.2 %collective-permute-start.20 = (f32[7,128,128]{2,1,0:T(8,128)}, f32[7,128,128]{2,1,0:T(8,128)}, u32[]{:S(2)}, u32[]{:S(2)}) collective-permute-start(f32[7,128,128]{2,1,0:T(8,128)} %param.18), channel_id=1, source_target_pairs={{0,1},{1,2},{2,3},{3,4},{4,5},{5,6},{6,7},{7,8},{8,9},{9,10},{10,1... | collective-permute-start | bytes 1376264 | tf_op jit(solution)/shard_map/cond/branch_2_fun/ppermute | solution.py:506
  40.9 10.0 %collective-permute-start.21 = (f32[7,72,128]{2,1,0:T(8,128)S(1)}, f32[7,72,128]{2,1,0:T(8,128)}, u32[]{:S(2)}, u32[]{:S(2)}) collective-permute-start(f32[7,72,128]{2,1,0:T(8,128)S(1)} %get-tuple-element.87), channel_id=1, source_target_pairs={{0,2},{1,3},{2,4},{3,5},{4,6},{5,7},{6,8},{7,9},{8,10},{9,11},{10,... | collective-permute-start | bytes 774152 | tf_op jit(solution)/shard_map/cond/branch_2_fun/ppermute | solution.py:506
  51.0 8.3 %copy-start = (f32[7,32,128]{2,1,0:T(8,128)S(1)}, f32[7,32,128]{2,1,0:T(8,128)}, u32[]{:S(2)}) copy-start(f32[7,32,128]{2,1,0:T(8,128)} %get-tuple-element.61.c0) | copy-start | bytes 344068
  51.0 8.4 %collective-permute-start.27 = (f32[7,32,128]{2,1,0:T(8,128)S(1)}, f32[7,32,128]{2,1,0:T(8,128)S(1)}, u32[]{:S(2)}, u32[]{:S(2)}) collective-permute-start(f32[7,32,128]{2,1,0:T(8,128)S(1)} %copy-done.1), channel_id=1, source_target_pairs={{0,192},{64,0},{128,64},{192,128},{1,193},{65,1},{129,65},{193,129... | collective-permute-start | bytes 344072 | tf_op jit(solution)/shard_map/ppermute | solution.py:540
  55.8 17.1 %all-to-all-start = ((f32[4,7,48,128]{3,2,1,0:T(8,128)}), f32[4,7,48,128]{3,2,1,0:T(8,128)S(1)}, u32[]{:S(2)}, u32[]{:S(2)}) async-start(f32[4,7,48,128]{3,2,1,0:T(8,128)} %select.19), calls=%async_computation | async-start | bytes 1376256 | tf_op jit(solution)/shard_map/all_to_all | solution.py:555
  59.4 13.5 %collective-permute-start.28 = (f32[4,7,8,128]{3,2,1,0:T(8,128)S(1)}, f32[4,7,8,128]{3,2,1,0:T(8,128)S(1)}, u32[]{:S(2)}, u32[]{:S(2)}) collective-permute-start(f32[4,7,8,128]{3,2,1,0:T(8,128)S(1)} %pad_maximum_fusion), channel_id=1, source_target_pairs={{0,64},{64,128},{128,192},{192,1},{1,65},{65,129},{129,193},{193,2... | collective-permute-start | bytes 344072 | tf_op jit(solution)/shard_map/ppermute | solution.py:546
  60.9 12.0 %collective-permute-start.29 = (f32[4,7,8,128]{3,2,1,0:T(8,128)S(1)}, f32[4,7,8,128]{3,2,1,0:T(8,128)S(1)}, u32[]{:S(2)}, u32[]{:S(2)}) collective-permute-start(f32[4,7,8,128]{3,2,1,0:T(8,128)S(1)} %pad_maximum_fusion.1), channel_id=1, source_target_pairs={{0,255},{64,0},{128,64},{192,128},{1,192},{65,1},{129,65},{193,129... | collective-permute-start | bytes 344072 | tf_op jit(solution)/shard_map/ppermute | solution.py:547

commit v2 on v0

--- a/solution.py
+++ b/solution.py
@@ -7,6 +7,7 @@
 from jax.experimental.pallas import tpu as pltpu
 from jax.sharding import Mesh
 from jax.sharding import PartitionSpec as P
+
 
 LON = ("x", "z", "core")
 NLON = 8192
@@ -20,7 +21,6 @@
 TOTAL = 2 * HALF
 SCALE = 1.0e-4
 F32 = jnp.float32
-HIGHEST = lax.Precision.HIGHEST
 E, W, N, S, NE, SW, NW, SE, DIAG = range(9)
 MULT, IPIV, LOWER, UPPER = range(4)
 
@@ -123,24 +123,37 @@
     return y, jnp.broadcast_to(ratio, (8, 128))
 
 
-def pack_body(place, rhs, surface, east, north, neast, nwest, land, out, *chunks):
+def pack_body(rhs, surface, east, north, neast, nwest, land, out):
     for k, ref in enumerate((rhs, surface, east, north, neast, nwest)):
         out[k] = ref[...].T
     out[6] = land[...].astype(F32).T
-    for step, chunk in enumerate(chunks):
-        start = pl.multiple_of(OWN * ((place[0] + step) & 3), OWN)
-        chunk[...] = out[:, pl.ds(start, OWN), :]
+
+
+def window_body(before, packed, after, out):
+    for place in range(7):
+        wide = jnp.concatenate([before[place], packed[place], after[place]], axis=0)
+        for part in range(4):
+            out[part, place] = wide[OWN * part : OWN * part + WIDE, :]
 
 
 def select_body(shift, low, main, high, out):
     i = lax.broadcasted_iota(jnp.int32, (PAD, COLS + 2 * SIDE), 0)
     u = lax.broadcasted_iota(jnp.int32, (PAD, COLS + 2 * SIDE), 1)
     reach = shift[0] + GHOST + SIDE
-    plain = jnp.where(u == reach - i, 1.0, 0.0)
-    moved = jnp.where(u == reach - 1 - i, 1.0, 0.0)
+    plain = jnp.where(u == reach - i, 1.0, 0.0).astype(jnp.bfloat16)
+    moved = jnp.where(u == reach - 1 - i, 1.0, 0.0).astype(jnp.bfloat16)
+
+    def pick(choice, values):
+        return jnp.dot(choice, values, preferred_element_type=F32)
+
     for place, source in enumerate((0, 1, 2, 3, 5, 4, 6)):
         both = jnp.concatenate([low[source], main[source], high[source]], axis=0)
-        facing = jnp.dot(moved if source == 2 else plain, both, precision=HIGHEST, preferred_element_type=F32)
+        top = both.astype(jnp.bfloat16)
+        rest = both - top.astype(F32)
+        middle = rest.astype(jnp.bfloat16)
+        bottom = (rest - middle.astype(F32)).astype(jnp.bfloat16)
+        choice = moved if source == 2 else plain
+        facing = (pick(choice, top) + pick(choice, middle)) + pick(choice, bottom)
         for part in range(4):
             out[part, place] = facing[OWN * part : OWN * part + WIDE, :]
 
@@ -291,16 +304,14 @@
     return lambda t: ref[(*index, t)]
 
 
-def first_body(lat, c0, c1, c2, c3, lefts, rights, facing, coef, lines, below_mat, above_mat, fold, r0, v_ref, w_ref, gram, raw, grid, y_buf, g_buf, vp, ve, vw, highs, lows):
+def first_body(own, facing, coef, lines, below_mat, above_mat, fold, r0, v_ref, w_ref, gram, raw, grid, y_buf, g_buf, vp, ve, vw, highs, lows):
     s_id = lax.broadcasted_iota(jnp.int32, (8, 128), 0)
     zero = jnp.zeros((8, 128), F32)
     gap = jnp.zeros((64 - WIDE, 128), F32)
     for place in range(7):
-        for step, chunk in enumerate((c0, c1, c2, c3)):
-            source = (lat[0] - step) & 3
-            left, right = lefts[(step - 1) % 4, place], rights[(step + 1) % 4, place]
-            full = jnp.concatenate([left, chunk[place], right, gap, facing[source, place], gap], axis=0)
-            raw[place, pl.ds(pl.multiple_of(128 * source, 128), 128), :] = full.T
+        for source in range(4):
+            full = jnp.concatenate([own[source, place], gap, facing[source, place], gap], axis=0)
+            raw[place, 128 * source : 128 * source + 128, :] = full.T
         for t in range(STEPS):
             grid[place, t + 1] = raw[place, pl.ds(t, 8, stride=STEPS), :]
     top_north = grid[3, STEPS]
@@ -340,7 +351,6 @@
         return 0
 
     lax.fori_loop(0, STEPS, weigh, 0, unroll=2)
-    surface = grid[1, STEPS]
     o = top_ocean
     coef[DIAG, STEPS - 1] = coef[DIAG, STEPS - 1] + o * fold_open
 
@@ -523,27 +533,27 @@
     return lax.cond(odd == 0, even_branch, odd_branch, block)
 
 
+def swap_lat(pieces):
+    return lax.all_to_all(pieces, "lat", split_axis=0, concat_axis=0, tiled=True)
+
+
 def shards(right_side, surface_term, east, north, neast, nwest, land_sea, fold_map):
-    lat = lax.axis_index("lat").reshape(1)
     offset = (fold_map[0] + COLS * lax.axis_index(LON)) % NLON
     centre = ((offset - COLS // 2) % NLON) // COLS
     shift = (offset - COLS // 2) % COLS + COLS // 2
     smem = pl.BlockSpec(memory_space=pltpu.SMEM)
     whole = pl.BlockSpec(memory_space=pltpu.VMEM)
-    packed, *chunks = pl.pallas_call(
-        pack_body,
-        in_specs=[smem] + [whole] * 7,
-        out_shape=(shape(7, COLS, 128),) + (shape(7, OWN, 128),) * 4,
-        name="pack",
-    )(lat, right_side, surface_term, east, north, neast, nwest, land_sea)
-    for step in range(1, 4):
-        chunks[step] = lax.ppermute(chunks[step], "lat", [(i, (i + step) % 4) for i in range(4)])
-    low, main, high = strips(reflect(packed, centre // 2), centre % 2)
-    where = [64 * (k % 4) + k // 4 for k in range(256)]
-    lefts = jnp.stack([c[:, OWN - GHOST :] for c in chunks])
-    rights = jnp.stack([c[:, :GHOST] for c in chunks])
-    lefts = lax.ppermute(lefts, ("lat", *LON), [(where[k], where[(k + 1) % 256]) for k in range(256)])
-    rights = lax.ppermute(rights, ("lat", *LON), [(where[k], where[k - 1]) for k in range(256)])
+    packed = pl.pallas_call(pack_body, out_shape=shape(7, COLS, 128), name="pack")(
+        right_side, surface_term, east, north, neast, nwest, land_sea
+    )
+    before = ring(packed[:, COLS - GHOST :], 1)
+    after = ring(packed[:, :GHOST], -1)
+    block = reflect(packed, centre // 2)
+    own = pl.pallas_call(window_body, out_shape=shape(4, 7, WIDE, 128), name="window", compiler_params=params())(
+        before, packed, after
+    )
+    own = swap_lat(own)
+    low, main, high = strips(block, centre % 2)
     windows = pl.pallas_call(
         select_body,
         in_specs=[smem] + [whole] * 3,
@@ -551,7 +561,7 @@
         name="select",
         compiler_params=params(),
     )(shift.reshape(1), low, main, high)
-    facing = lax.all_to_all(windows, "lat", split_axis=0, concat_axis=0, tiled=True)
+    facing = swap_lat(windows)
     coef, lines, below_mat, above_mat, fold, r0, v1, w1, gram = pl.pallas_call(
         first_body,
         out_shape=(
@@ -566,10 +576,9 @@
             shape(512, 128),
         ),
         scratch_shapes=[vmem(7, 512, 128), vmem(7, STEPS + 2, 8, 128), *SCRATCH],
-        in_specs=[smem] + [whole] * 7,
         name="phase_one",
         compiler_params=params(),
-    )(lat, *chunks, lefts, rights, facing)
+    )(own, facing)
     sums = all_sums(gram)
     r4, y1, v2, w2, gram = pl.pallas_call(
         second_body,
@@ -592,7 +601,7 @@
         name="combine",
         compiler_params=params(),
     )(sums, y1, r4, v1, w1, v2, w2)
-    columns = lax.all_to_all(pieces, "lat", split_axis=0, concat_axis=0, tiled=True)
+    columns = swap_lat(pieces)
     return pl.pallas_call(unpack_body, out_shape=(shape(128, COLS), shape(128, COLS)), name="unpack")(columns)
 
 

time: 203 us -> 156 us (0.77)
  starting transfers between devices: 81 us -> 19.1 us
  waiting for transfers between devices: 20.2 us -> 31.6 us
  blocking collectives: 58.7 us -> 65.3 us
    ppermute x5 -> x0, starting transfers between devices: 61.3 us -> none  [the longest x3 37.4 us: shards(): lax.ppermute(chunks[step], 'lat', [(i, (i + step) % 4) for i in range(4)])]
    all_to_all x1 -> x2, blocking collectives: 7.89 us -> 19.7 us  [swap_lat(): lax.all_to_all(pieces, 'lat', split_axis=0, concat_axis=0, tiled=True)]
    ppermute x1, waiting for transfers between devices: 10.9 us -> 20.2 us  [branch(): lax.ppermute(b, LON, [(d, (2 * q - d) % 64) for d in range(64)])]
    all_to_all x2, blocking collectives: 50.8 us -> 45.6 us  [all_sums(): lax.all_to_all(gram, ('lat', *LON), split_axis=0, concat_axis=0, tiled=True)]
    ppermute x2 -> x4, starting transfers between devices: 9.01 us -> 4.19 us  [ring(): return lax.ppermute(block, LON, [(d, (d + step) % 64) for d in range(64)])]
    all_to_all x1, waiting for transfers between devices: 0.01 us -> 4.72 us  [swap_lat(): lax.all_to_all(pieces, 'lat', split_axis=0, concat_axis=0, tiled=True)]
    ppermute x5 -> x0, waiting for transfers between devices: 4.49 us -> none  [the longest x1 4.48 us: shards(): lax.ppermute(rights, ('lat', *LON), [(where[k], where[k - 1]) for k in ra...]
    ppermute x1, starting transfers between devices: 6.64 us -> 10.8 us  [branch(): lax.ppermute(b, LON, [(d, (2 * q - d) % 64) for d in range(64)])]
  transfers between devices with their start and end apart: 9 -> 6, of which waited for: 4 -> 5; matrix products, arithmetic and copies ran while one was open for 1% -> 1% of each run, Pallas kernels for 2% -> 0%
where the time goes in v2:
time: 156 us; the launch traced here: 155 us
  blocking collectives  65.3 us (42%)
  Pallas kernels  35.9 us (23%)
  waiting for transfers between devices  31.6 us (20%)
  starting transfers between devices  19.1 us (12%)
  local copies, waits for them, and re-layouts  2.13 us (1%)
    all_to_all x2, blocking collectives, all_sums(): lax.all_to_all(gram, ('lat', *LON), split_axis=0, concat_axis=0, tiled=True)  45.6 us
    ppermute x1, waiting for transfers between devices, branch(): lax.ppermute(b, LON, [(d, (2 * q - d) % 64) for d in range(64)])  20.2 us
    all_to_all x2, blocking collectives, swap_lat(): lax.all_to_all(pieces, 'lat', split_axis=0, concat_axis=0, tiled=True)  19.7 us
    pallas_call x1, Pallas kernels, shards(): pl.pallas_call(second_body, out_shape=(shape(*FIELD), shape(8, 128), shap...  14.4 us
    pallas_call x1, Pallas kernels, shards(): pl.pallas_call(first_body, out_shape=(shape(9, *FIELD), shape(4, STEPS +...  13.7 us
    ppermute x1, starting transfers between devices, branch(): lax.ppermute(b, LON, [(d, (2 * q - d) % 64) for d in range(64)])  10.8 us
    ppermute x4, waiting for transfers between devices, ring(): return lax.ppermute(block, LON, [(d, (d + step) % 64) for d in range(64)])  6.68 us
    all_to_all x1, waiting for transfers between devices, swap_lat(): lax.all_to_all(pieces, 'lat', split_axis=0, concat_axis=0, tiled=True)  4.72 us
  transfers between devices with their start and end apart: 6, of which 5 were waited for; matrix products, arithmetic and copies ran while one was open for 1% of the time, Pallas kernels for 0%

profile of v2, /device:TPU:1, one launch (start us, length us, event | category | flops | bytes accessed | tf_op | source)
XLA Modules:
  0.0 155.5 jit_solution(570895377137403526)
XLA Ops:
  1.4 1.2 pack.1.packed
  2.6 31.0 %conditional.2 = (f32[7,128,128]{2,1,0:T(8,128)}) conditional(s32[]{:T(128)} %clamp.3, f32[7,128,128]{2,1,0:T(8,128)S(1)} %pack.1.packed, f32[7,128,128]{2,1,0:T(8,128)S(1)} %pack.1.packed, f32[7,128,128]{2,1,0:T(8,128)S(1)} %pack.1.packed, f32[7,128,128]{2,1,0:T(8,128)S(1)} %pack.1.packed, ...), branch_computations={%region_0.1_spmd, %region_1.2_spmd, %region_2.3_spmd, %region_3.4_... | conditional | bytes 1835056 | solution.py:523
  2.6 10.8 %collective-permute-start.24 = (f32[7,128,128]{2,1,0:T(8,128)S(1)}, f32[7,128,128]{2,1,0:T(8,128)}, u32[]{:S(2)}, u32[]{:S(2)}) collective-permute-start(f32[7,128,128]{2,1,0:T(8,128)S(1)} %param.24), channel_id=1, source_target_pairs={{0,48},{1,47},{2,46},{3,45},{4,44},{5,43},{6,42},{7,41},{8,40},{9,... | collective-permute-start | bytes 1376264 | tf_op jit(solution)/shard_map/cond/branch_24_fun/ppermute | solution.py:521
  13.4 20.2 %collective-permute-done.24 = f32[7,128,128]{2,1,0:T(8,128)} collective-permute-done((f32[7,128,128]{2,1,0:T(8,128)S(1)}, f32[7,128,128]{2,1,0:T(8,128)}, u32[]{:S(2)}, u32[]{:S(2)}) %collective-permute-start.24) | collective-permute-done | bytes 458784 | tf_op jit(solution)/shard_map/cond/branch_24_fun/ppermute | solution.py:521
  33.6 9.3 %conditional.3 = (f32[7,72,128]{2,1,0:T(8,128)}, f32[7,128,128]{2,1,0:T(8,128)S(1)}, f32[7,72,128]{2,1,0:T(8,128)}) conditional(s32[]{:T(128)} %convert_element_type.3, f32[7,128,128]{2,1,0:T(8,128)} %get-tuple-element.115, f32[7,128,128]{2,1,0:T(8,128)} %get-tuple-element.115), branch_computations={%region_32.33_spmd, %region_33.34_spmd} | conditional | bytes 4014184 | solution.py:533
  33.6 1.1 fusion.1
  34.7 2.4 %collective-permute-start.35 = (f32[7,72,128]{2,1,0:T(8,128)S(1)}, f32[7,72,128]{2,1,0:T(8,128)}, u32[]{:S(2)}, u32[]{:S(2)}) collective-permute-start(f32[7,72,128]{2,1,0:T(8,128)S(1)} %get-tuple-element.105), channel_id=1, source_target_pairs={{0,1},{1,2},{2,3},{3,4},{4,5},{5,6},{6,7},{7,8},{8,9},{9,10},{10,1... | collective-permute-start | bytes 774152 | tf_op jit(solution)/shard_map/cond/branch_1_fun/ppermute | solution.py:516
  37.1 1.0 copy.46
  38.1 2.3 %collective-permute-done.35 = f32[7,72,128]{2,1,0:T(8,128)} collective-permute-done((f32[7,72,128]{2,1,0:T(8,128)S(1)}, f32[7,72,128]{2,1,0:T(8,128)}, u32[]{:S(2)}, u32[]{:S(2)}) %collective-permute-start.35) | collective-permute-done | bytes 258080 | tf_op jit(solution)/shard_map/cond/branch_1_fun/ppermute | solution.py:516
  40.3 2.6 %collective-permute-done.34 = f32[7,72,128]{2,1,0:T(8,128)} collective-permute-done((f32[7,72,128]{2,1,0:T(8,128)S(1)}, f32[7,72,128]{2,1,0:T(8,128)}, u32[]{:S(2)}, u32[]{:S(2)}) %collective-permute-start.34) | collective-permute-done | bytes 258080 | tf_op jit(solution)/shard_map/cond/branch_1_fun/ppermute | solution.py:516
  42.9 2.9 %select.17 = f32[4,7,48,128]{3,2,1,0:T(8,128)} custom-call(s32[1]{0:T(128)} %bitcast.1.shift, f32[7,72,128]{2,1,0:T(8,128)} %get-tuple-element.86.low, f32[7,128,128]{2,1,0:T(8,128)S(1)} %get-tuple-element.87.main, f32[7,72,128]{2,1,0:T(8,128)} %get-tuple-element.88.high), custom_call_target="tpu_custom_call" | custom-call | tf_op jit(solution)/shard_map/select/pallas_call | solution.py:557
  45.8 4.2 %all-to-all-start.1 = ((f32[4,7,48,128]{3,2,1,0:T(8,128)}), f32[4,7,48,128]{3,2,1,0:T(8,128)S(1)}, u32[]{:S(2)}, u32[]{:S(2)}) async-start(f32[4,7,48,128]{3,2,1,0:T(8,128)} %select.17), calls=%async_computation.1 | async-start | bytes 1376256 | tf_op jit(solution)/shard_map/all_to_all | solution.py:537
  50.0 0.1 collective-permute-start.37
  50.1 1.7 %collective-permute-start.36 = (f32[7,8,128]{2,1,0:T(8,128)S(1)}, f32[7,8,128]{2,1,0:T(8,128)S(1)}, u32[]{:S(2)}, u32[]{:S(2)}) collective-permute-start(f32[7,8,128]{2,1,0:T(8,128)S(1)} %get-tuple-element.108), channel_id=1, source_target_pairs={{0,1},{1,2},{2,3},{3,4},{4,5},{5,6},{6,7},{7,8},{8,9},{9,10},{10,1... | collective-permute-start | bytes 86024 | tf_op jit(solution)/shard_map/ppermute | solution.py:516
  51.8 1.8 %collective-permute-done.37.after = f32[7,8,128]{2,1,0:T(8,128)S(1)} collective-permute-done((f32[7,8,128]{2,1,0:T(8,128)S(1)}, f32[7,8,128]{2,1,0:T(8,128)S(1)}, u32[]{:S(2)}, u32[]{:S(2)}) %collective-permute-start.37) | collective-permute-done | bytes 28704 | tf_op jit(solution)/shard_map/ppermute | solution.py:516
  53.7 4.7 %all-to-all-done.1.facing = f32[4,7,48,128]{3,2,1,0:T(8,128)S(1)} async-done(((f32[4,7,48,128]{3,2,1,0:T(8,128)}), f32[4,7,48,128]{3,2,1,0:T(8,128)S(1)}, u32[]{:S(2)}, u32[]{:S(2)}) %all-to-all-start.1) | async-done | bytes 688160 | tf_op jit(solution)/shard_map/all_to_all | solution.py:537
  58.4 11.8 %all_to_all.37.own = f32[4,7,48,128]{3,2,1,0:T(8,128)S(1)} all-to-all(f32[4,7,48,128]{3,2,1,0:T(8,128)S(1)} %window.1), channel_id=1, replica_groups=mesh['lat'=4,'x'=4,'z'=8,'core'=2] {'lat'}, dimensions={0} | all-to-all | bytes 1376256 | tf_op jit(solution)/shard_map/all_to_all | solution.py:537
  70.2 13.7 %phase_one.1 = (f32[9,64,8,128]{3,2,1,0:T(8,128)S(1)}, f32[4,72,8,128]{3,2,1,0:T(8,128)S(1)}, f32[16,8,128]{2,1,0:T(8,128)S(1)}, f32[16,8,128]{2,1,0:T(8,128)S(1...) custom-call(f32[4,7,48,128]{3,2,1,0:T(8,128)S(1)} %all_to_all.37.own, ...), custom_call_target="tpu_custom_call" | custom-call | tf_op jit(solution)/shard_map/phase_one/pallas_call | solution.py:565
  83.9 24.4 %all_to_all.38 = f32[256,2,128]{2,1,0:T(2,128)S(1)} all-to-all(f32[256,2,128]{2,1,0:T(2,128)S(1)} %bitcast.10), channel_id=1, replica_groups=mesh['lat'=4,'x'=4,'z'=8,'core'=2] {'lat','x','z','core'}, dimensions={0} | all-to-all | bytes 524288 | tf_op jit(solution)/shard_map/all_to_all | solution.py:512
  108.3 14.4 %phase_two.1 = (f32[64,8,128]{2,1,0:T(8,128)S(1)}, f32[8,128]{1,0:T(8,128)S(1)}, f32[4,64,8,128]{3,2,1,0:T(8,128)S(1)}, f32[4,64,8,128]{3,2,1,0:T(8,128)S(1)}, f32[512,128]{1,0:T(8,128)S(1)}) custom-call(f32[512,128]{1,0:T(8,128)S(1)} %bitcast.8, f32[9,64,8,128]{3,2,1,0:T(8,128)S(1)} %get-tuple-element.90.coef, ...), custom_call_target="tpu_custom_call" | custom-call | tf_op jit(solution)/shard_map/phase_two/pallas_call | solution.py:583
  122.7 21.2 %all_to_all.39 = f32[256,2,128]{2,1,0:T(2,128)S(1)} all-to-all(f32[256,2,128]{2,1,0:T(2,128)S(1)} %bitcast.9), channel_id=1, replica_groups=mesh['lat'=4,'x'=4,'z'=8,'core'=2] {'lat','x','z','core'}, dimensions={0} | all-to-all | bytes 524288 | tf_op jit(solution)/shard_map/all_to_all | solution.py:512
  143.9 2.0 %combine.1 = f32[4,2,32,128]{3,2,1,0:T(8,128)S(1)} custom-call(f32[512,128]{1,0:T(8,128)S(1)} %bitcast.7, f32[8,128]{1,0:T(8,128)S(1)} %get-tuple-element.99.y1, f32[64,8,128]{2,1,0:T(8,128)S(1)} %get-tuple-element.100.r_ref, f32[4,64,8,128]{3,2,1,0:T(8,128)S(1)} %get-tuple-element.96.v1, f32[4,64,8,128]{3,2,1,0:T(8,128)S(1)} %get-tuple-element.97.w1, ...), custom_call_target="tpu_custom_call" | custom-call | tf_op jit(solution)/shard_map/combine/pallas_call | solution.py:597
  145.9 7.9 %all_to_all.40.recv = f32[4,2,32,128]{3,2,1,0:T(8,128)} all-to-all(f32[4,2,32,128]{3,2,1,0:T(8,128)S(1)} %combine.1), channel_id=1, replica_groups=mesh['lat'=4,'x'=4,'z'=8,'core'=2] {'lat'}, dimensions={0} | all-to-all | bytes 262144 | tf_op jit(solution)/shard_map/all_to_all | solution.py:537
  153.8 1.7 %unpack.1 = (f32[128,128]{1,0:T(8,128)}, f32[128,128]{1,0:T(8,128)}) custom-call(f32[4,2,32,128]{3,2,1,0:T(8,128)} %all_to_all.40.recv), custom_call_target="tpu_custom_call" | custom-call | tf_op jit(solution)/shard_map/unpack/pallas_call | solution.py:605
  (4 shorter events, 0.1 us)
Async XLA Ops:
  2.6 30.9 %collective-permute-start.24 = (f32[7,128,128]{2,1,0:T(8,128)S(1)}, f32[7,128,128]{2,1,0:T(8,128)}, u32[]{:S(2)}, u32[]{:S(2)}) collective-permute-start(f32[7,128,128]{2,1,0:T(8,128)S(1)} %param.24), channel_id=1, source_target_pairs={{0,48},{1,47},{2,46},{3,45},{4,44},{5,43},{6,42},{7,41},{8,40},{9,... | collective-permute-start | bytes 1376264 | tf_op jit(solution)/shard_map/cond/branch_24_fun/ppermute | solution.py:521
  34.7 5.7 %collective-permute-start.35 = (f32[7,72,128]{2,1,0:T(8,128)S(1)}, f32[7,72,128]{2,1,0:T(8,128)}, u32[]{:S(2)}, u32[]{:S(2)}) collective-permute-start(f32[7,72,128]{2,1,0:T(8,128)S(1)} %get-tuple-element.105), channel_id=1, source_target_pairs={{0,1},{1,2},{2,3},{3,4},{4,5},{5,6},{6,7},{7,8},{8,9},{9,10},{10,1... | collective-permute-start | bytes 774152 | tf_op jit(solution)/shard_map/cond/branch_1_fun/ppermute | solution.py:516
  37.1 5.9 %collective-permute-start.34 = (f32[7,72,128]{2,1,0:T(8,128)S(1)}, f32[7,72,128]{2,1,0:T(8,128)}, u32[]{:S(2)}, u32[]{:S(2)}) collective-permute-start(f32[7,72,128]{2,1,0:T(8,128)S(1)} %get-tuple-element.106), channel_id=1, source_target_pairs={{0,63},{1,0},{2,1},{3,2},{4,3},{5,4},{6,5},{7,6},{8,7},{9,8},{10,9... | collective-permute-start | bytes 774152 | tf_op jit(solution)/shard_map/cond/branch_1_fun/ppermute | solution.py:516
  45.8 12.6 %all-to-all-start.1 = ((f32[4,7,48,128]{3,2,1,0:T(8,128)}), f32[4,7,48,128]{3,2,1,0:T(8,128)S(1)}, u32[]{:S(2)}, u32[]{:S(2)}) async-start(f32[4,7,48,128]{3,2,1,0:T(8,128)} %select.17), calls=%async_computation.1 | async-start | bytes 1376256 | tf_op jit(solution)/shard_map/all_to_all | solution.py:537
  50.0 3.7 %collective-permute-start.37 = (f32[7,8,128]{2,1,0:T(8,128)S(1)}, f32[7,8,128]{2,1,0:T(8,128)S(1)}, u32[]{:S(2)}, u32[]{:S(2)}) collective-permute-start(f32[7,8,128]{2,1,0:T(8,128)S(1)} %get-tuple-element.107), channel_id=1, source_target_pairs={{0,63},{1,0},{2,1},{3,2},{4,3},{5,4},{6,5},{7,6},{8,7},{9,8},{10,9... | collective-permute-start | bytes 86024 | tf_op jit(solution)/shard_map/ppermute | solution.py:516
  50.1 3.6 %collective-permute-start.36 = (f32[7,8,128]{2,1,0:T(8,128)S(1)}, f32[7,8,128]{2,1,0:T(8,128)S(1)}, u32[]{:S(2)}, u32[]{:S(2)}) collective-permute-start(f32[7,8,128]{2,1,0:T(8,128)S(1)} %get-tuple-element.108), channel_id=1, source_target_pairs={{0,1},{1,2},{2,3},{3,4},{4,5},{5,6},{6,7},{7,8},{8,9},{9,10},{10,1... | collective-permute-start | bytes 86024 | tf_op jit(solution)/shard_map/ppermute | solution.py:516

commit v3 on v2

--- a/solution.py
+++ b/solution.py
@@ -22,7 +22,8 @@
 SCALE = 1.0e-4
 F32 = jnp.float32
 E, W, N, S, NE, SW, NW, SE, DIAG = range(9)
-MULT, IPIV, LOWER, UPPER = range(4)
+MULT, IPIV, LOWER, UPPER, RISE, FALL = range(6)
+SPAN = 8
 
 
 SIDE = 72
@@ -183,20 +184,25 @@
 def line_solve(load, lines, below_mat, above_mat, y_buf, g_buf, finish):
     zero = jnp.zeros((8, 128), F32)
 
-    def forward(t, y):
-        y = load(t) + lines[MULT, t] * y
-        y_buf[t] = y
-        return y
-
-    lax.fori_loop(0, STEPS, forward, zero, unroll=8)
-
-    def backward(k, x):
-        t = STEPS - 1 - k
-        x = y_buf[t] * lines[IPIV, t] + lines[MULT, t + 1] * x
-        g_buf[t] = x
-        return x
-
-    lax.fori_loop(0, STEPS, backward, zero, unroll=8)
+    carried = zero
+    for start in range(0, STEPS, SPAN):
+        local = zero
+        before = carried
+        for t in range(start, start + SPAN):
+            local = load(t) + lines[MULT, t] * local if t > start else load(t)
+            y = local + lines[RISE, t] * before
+            y_buf[t] = y
+        carried = y
+    carried = zero
+    for start in range(STEPS - 1, -1, -SPAN):
+        local = zero
+        after = carried
+        for t in range(start, start - SPAN, -1):
+            scaled = y_buf[t] * lines[IPIV, t]
+            local = scaled + lines[MULT, t + 1] * local if t < start else scaled
+            x = local + lines[FALL, t] * after
+            g_buf[t] = x
+        carried = x
     first, last = g_buf[0], g_buf[STEPS - 1]
     below, above = zero, zero
     for k in range(8):
@@ -385,6 +391,14 @@
     lax.fori_loop(0, STEPS, pivots, (zero,) * 4, unroll=4)
     for t in range(STEPS, lines.shape[1]):
         lines[MULT, t] = zero
+    for start in range(0, STEPS, SPAN):
+        rise = lines[MULT, start]
+        fall = lines[MULT, start + SPAN]
+        for k in range(SPAN):
+            lines[RISE, start + k] = rise
+            lines[FALL, start + SPAN - 1 - k] = fall
+            rise = rise * lines[MULT, start + k + 1]
+            fall = fall * lines[MULT, start + SPAN - 1 - k]
 
     def respond(k, carry):
         low, up, source = carry
@@ -566,7 +580,7 @@
         first_body,
         out_shape=(
             shape(9, *FIELD),
-            shape(4, STEPS + 8, 8, 128),
+            shape(6, STEPS + 8, 8, 128),
             shape(16, 8, 128),
             shape(16, 8, 128),
             shape(8, 128),

time: 156 us -> 154 us (0.987)
  Pallas kernels: 35.9 us -> 33.7 us
where the time goes in v3:
time: 154 us; the launch traced here: 153 us
  blocking collectives  65.3 us (42%)
  Pallas kernels  33.7 us (22%)
  waiting for transfers between devices  31.6 us (21%)
  starting transfers between devices  19.1 us (12%)
  local copies, waits for them, and re-layouts  2.13 us (1%)
    all_to_all x2, blocking collectives, all_sums(): lax.all_to_all(gram, ('lat', *LON), split_axis=0, concat_axis=0, tiled=True)  45.6 us
    ppermute x1, waiting for transfers between devices, branch(): lax.ppermute(b, LON, [(d, (2 * q - d) % 64) for d in range(64)])  20.2 us
    all_to_all x2, blocking collectives, swap_lat(): lax.all_to_all(pieces, 'lat', split_axis=0, concat_axis=0, tiled=True)  19.7 us
    pallas_call x1, Pallas kernels, shards(): pl.pallas_call(second_body, out_shape=(shape(*FIELD), shape(8, 128), shap...  13.2 us
    pallas_call x1, Pallas kernels, shards(): pl.pallas_call(first_body, out_shape=(shape(9, *FIELD), shape(6, STEPS +...  12.6 us
    ppermute x1, starting transfers between devices, branch(): lax.ppermute(b, LON, [(d, (2 * q - d) % 64) for d in range(64)])  10.8 us
    ppermute x4, waiting for transfers between devices, ring(): return lax.ppermute(block, LON, [(d, (d + step) % 64) for d in range(64)])  6.68 us
    all_to_all x1, waiting for transfers between devices, swap_lat(): lax.all_to_all(pieces, 'lat', split_axis=0, concat_axis=0, tiled=True)  4.72 us
  transfers between devices with their start and end apart: 6, of which 5 were waited for; matrix products, arithmetic and copies ran while one was open for 1% of the time, Pallas kernels for 0%

profile of v3, /device:TPU:1, one launch (start us, length us, event | category | flops | bytes accessed | tf_op | source)
XLA Modules:
  0.0 153.2 jit_solution(570322557559591104)
XLA Ops:
  1.4 1.2 pack.1.packed
  2.6 31.0 %conditional.2 = (f32[7,128,128]{2,1,0:T(8,128)}) conditional(s32[]{:T(128)} %clamp.3, f32[7,128,128]{2,1,0:T(8,128)S(1)} %pack.1.packed, f32[7,128,128]{2,1,0:T(8,128)S(1)} %pack.1.packed, f32[7,128,128]{2,1,0:T(8,128)S(1)} %pack.1.packed, f32[7,128,128]{2,1,0:T(8,128)S(1)} %pack.1.packed, ...), branch_computations={%region_0.1_spmd, %region_1.2_spmd, %region_2.3_spmd, %region_3.4_... | conditional | bytes 1835056 | solution.py:537
  2.6 10.8 %collective-permute-start.24 = (f32[7,128,128]{2,1,0:T(8,128)S(1)}, f32[7,128,128]{2,1,0:T(8,128)}, u32[]{:S(2)}, u32[]{:S(2)}) collective-permute-start(f32[7,128,128]{2,1,0:T(8,128)S(1)} %param.24), channel_id=1, source_target_pairs={{0,48},{1,47},{2,46},{3,45},{4,44},{5,43},{6,42},{7,41},{8,40},{9,... | collective-permute-start | bytes 1376264 | tf_op jit(solution)/shard_map/cond/branch_24_fun/ppermute | solution.py:535
  13.4 20.2 %collective-permute-done.24 = f32[7,128,128]{2,1,0:T(8,128)} collective-permute-done((f32[7,128,128]{2,1,0:T(8,128)S(1)}, f32[7,128,128]{2,1,0:T(8,128)}, u32[]{:S(2)}, u32[]{:S(2)}) %collective-permute-start.24) | collective-permute-done | bytes 458784 | tf_op jit(solution)/shard_map/cond/branch_24_fun/ppermute | solution.py:535
  33.6 9.3 %conditional.3 = (f32[7,72,128]{2,1,0:T(8,128)}, f32[7,128,128]{2,1,0:T(8,128)S(1)}, f32[7,72,128]{2,1,0:T(8,128)}) conditional(s32[]{:T(128)} %convert_element_type.3, f32[7,128,128]{2,1,0:T(8,128)} %get-tuple-element.115, f32[7,128,128]{2,1,0:T(8,128)} %get-tuple-element.115), branch_computations={%region_32.33_spmd, %region_33.34_spmd} | conditional | bytes 4014184 | solution.py:547
  33.6 1.1 fusion.1
  34.7 2.4 %collective-permute-start.35 = (f32[7,72,128]{2,1,0:T(8,128)S(1)}, f32[7,72,128]{2,1,0:T(8,128)}, u32[]{:S(2)}, u32[]{:S(2)}) collective-permute-start(f32[7,72,128]{2,1,0:T(8,128)S(1)} %get-tuple-element.105), channel_id=1, source_target_pairs={{0,1},{1,2},{2,3},{3,4},{4,5},{5,6},{6,7},{7,8},{8,9},{9,10},{10,1... | collective-permute-start | bytes 774152 | tf_op jit(solution)/shard_map/cond/branch_1_fun/ppermute | solution.py:530
  37.1 1.0 copy.46
  38.1 2.3 %collective-permute-done.35 = f32[7,72,128]{2,1,0:T(8,128)} collective-permute-done((f32[7,72,128]{2,1,0:T(8,128)S(1)}, f32[7,72,128]{2,1,0:T(8,128)}, u32[]{:S(2)}, u32[]{:S(2)}) %collective-permute-start.35) | collective-permute-done | bytes 258080 | tf_op jit(solution)/shard_map/cond/branch_1_fun/ppermute | solution.py:530
  40.3 2.6 %collective-permute-done.34 = f32[7,72,128]{2,1,0:T(8,128)} collective-permute-done((f32[7,72,128]{2,1,0:T(8,128)S(1)}, f32[7,72,128]{2,1,0:T(8,128)}, u32[]{:S(2)}, u32[]{:S(2)}) %collective-permute-start.34) | collective-permute-done | bytes 258080 | tf_op jit(solution)/shard_map/cond/branch_1_fun/ppermute | solution.py:530
  42.9 2.9 %select.17 = f32[4,7,48,128]{3,2,1,0:T(8,128)} custom-call(s32[1]{0:T(128)} %bitcast.1.shift, f32[7,72,128]{2,1,0:T(8,128)} %get-tuple-element.86.low, f32[7,128,128]{2,1,0:T(8,128)S(1)} %get-tuple-element.87.main, f32[7,72,128]{2,1,0:T(8,128)} %get-tuple-element.88.high), custom_call_target="tpu_custom_call" | custom-call | tf_op jit(solution)/shard_map/select/pallas_call | solution.py:571
  45.8 4.2 %all-to-all-start.1 = ((f32[4,7,48,128]{3,2,1,0:T(8,128)}), f32[4,7,48,128]{3,2,1,0:T(8,128)S(1)}, u32[]{:S(2)}, u32[]{:S(2)}) async-start(f32[4,7,48,128]{3,2,1,0:T(8,128)} %select.17), calls=%async_computation.1 | async-start | bytes 1376256 | tf_op jit(solution)/shard_map/all_to_all | solution.py:551
  50.0 0.1 collective-permute-start.37
  50.1 1.7 %collective-permute-start.36 = (f32[7,8,128]{2,1,0:T(8,128)S(1)}, f32[7,8,128]{2,1,0:T(8,128)S(1)}, u32[]{:S(2)}, u32[]{:S(2)}) collective-permute-start(f32[7,8,128]{2,1,0:T(8,128)S(1)} %get-tuple-element.108), channel_id=1, source_target_pairs={{0,1},{1,2},{2,3},{3,4},{4,5},{5,6},{6,7},{7,8},{8,9},{9,10},{10,1... | collective-permute-start | bytes 86024 | tf_op jit(solution)/shard_map/ppermute | solution.py:530
  51.8 1.8 %collective-permute-done.37.after = f32[7,8,128]{2,1,0:T(8,128)S(1)} collective-permute-done((f32[7,8,128]{2,1,0:T(8,128)S(1)}, f32[7,8,128]{2,1,0:T(8,128)S(1)}, u32[]{:S(2)}, u32[]{:S(2)}) %collective-permute-start.37) | collective-permute-done | bytes 28704 | tf_op jit(solution)/shard_map/ppermute | solution.py:530
  53.7 4.7 %all-to-all-done.1.facing = f32[4,7,48,128]{3,2,1,0:T(8,128)S(1)} async-done(((f32[4,7,48,128]{3,2,1,0:T(8,128)}), f32[4,7,48,128]{3,2,1,0:T(8,128)S(1)}, u32[]{:S(2)}, u32[]{:S(2)}) %all-to-all-start.1) | async-done | bytes 688160 | tf_op jit(solution)/shard_map/all_to_all | solution.py:551
  58.4 11.8 %all_to_all.37.own = f32[4,7,48,128]{3,2,1,0:T(8,128)S(1)} all-to-all(f32[4,7,48,128]{3,2,1,0:T(8,128)S(1)} %window.1), channel_id=1, replica_groups=mesh['lat'=4,'x'=4,'z'=8,'core'=2] {'lat'}, dimensions={0} | all-to-all | bytes 1376256 | tf_op jit(solution)/shard_map/all_to_all | solution.py:551
  70.2 12.6 %phase_one.1 = (f32[9,64,8,128]{3,2,1,0:T(8,128)S(1)}, f32[6,72,8,128]{3,2,1,0:T(8,128)S(1)}, f32[16,8,128]{2,1,0:T(8,128)S(1)}, f32[16,8,128]{2,1,0:T(8,128)S(1...) custom-call(f32[4,7,48,128]{3,2,1,0:T(8,128)S(1)} %all_to_all.37.own, ...), custom_call_target="tpu_custom_call" | custom-call | tf_op jit(solution)/shard_map/phase_one/pallas_call | solution.py:579
  82.8 24.4 %all_to_all.38 = f32[256,2,128]{2,1,0:T(2,128)S(1)} all-to-all(f32[256,2,128]{2,1,0:T(2,128)S(1)} %bitcast.10), channel_id=1, replica_groups=mesh['lat'=4,'x'=4,'z'=8,'core'=2] {'lat','x','z','core'}, dimensions={0} | all-to-all | bytes 524288 | tf_op jit(solution)/shard_map/all_to_all | solution.py:526
  107.2 13.2 %phase_two.1 = (f32[64,8,128]{2,1,0:T(8,128)S(1)}, f32[8,128]{1,0:T(8,128)S(1)}, f32[4,64,8,128]{3,2,1,0:T(8,128)S(1)}, f32[4,64,8,128]{3,2,1,0:T(8,128)S(1)}, f32[512,128]{1,0:T(8,128)S(1)}) custom-call(f32[512,128]{1,0:T(8,128)S(1)} %bitcast.7, f32[9,64,8,128]{3,2,1,0:T(8,128)S(1)} %get-tuple-element.90.coef, ...), custom_call_target="tpu_custom_call" | custom-call | tf_op jit(solution)/shard_map/phase_two/pallas_call | solution.py:597
  120.4 21.2 %all_to_all.39 = f32[256,2,128]{2,1,0:T(2,128)S(1)} all-to-all(f32[256,2,128]{2,1,0:T(2,128)S(1)} %bitcast.9), channel_id=1, replica_groups=mesh['lat'=4,'x'=4,'z'=8,'core'=2] {'lat','x','z','core'}, dimensions={0} | all-to-all | bytes 524288 | tf_op jit(solution)/shard_map/all_to_all | solution.py:526
  141.7 2.0 %combine.1 = f32[4,2,32,128]{3,2,1,0:T(8,128)S(1)} custom-call(f32[512,128]{1,0:T(8,128)S(1)} %bitcast.8, f32[8,128]{1,0:T(8,128)S(1)} %get-tuple-element.99.y1, f32[64,8,128]{2,1,0:T(8,128)S(1)} %get-tuple-element.100.r_ref, f32[4,64,8,128]{3,2,1,0:T(8,128)S(1)} %get-tuple-element.96.v1, f32[4,64,8,128]{3,2,1,0:T(8,128)S(1)} %get-tuple-element.97.w1, ...), custom_call_target="tpu_custom_call" | custom-call | tf_op jit(solution)/shard_map/combine/pallas_call | solution.py:611
  143.7 7.9 %all_to_all.40.recv = f32[4,2,32,128]{3,2,1,0:T(8,128)} all-to-all(f32[4,2,32,128]{3,2,1,0:T(8,128)S(1)} %combine.1), channel_id=1, replica_groups=mesh['lat'=4,'x'=4,'z'=8,'core'=2] {'lat'}, dimensions={0} | all-to-all | bytes 262144 | tf_op jit(solution)/shard_map/all_to_all | solution.py:551
  151.6 1.7 %unpack.1 = (f32[128,128]{1,0:T(8,128)}, f32[128,128]{1,0:T(8,128)}) custom-call(f32[4,2,32,128]{3,2,1,0:T(8,128)} %all_to_all.40.recv), custom_call_target="tpu_custom_call" | custom-call | tf_op jit(solution)/shard_map/unpack/pallas_call | solution.py:619
  (4 shorter events, 0.1 us)
Async XLA Ops:
  2.6 30.9 %collective-permute-start.24 = (f32[7,128,128]{2,1,0:T(8,128)S(1)}, f32[7,128,128]{2,1,0:T(8,128)}, u32[]{:S(2)}, u32[]{:S(2)}) collective-permute-start(f32[7,128,128]{2,1,0:T(8,128)S(1)} %param.24), channel_id=1, source_target_pairs={{0,48},{1,47},{2,46},{3,45},{4,44},{5,43},{6,42},{7,41},{8,40},{9,... | collective-permute-start | bytes 1376264 | tf_op jit(solution)/shard_map/cond/branch_24_fun/ppermute | solution.py:535
  34.7 5.7 %collective-permute-start.35 = (f32[7,72,128]{2,1,0:T(8,128)S(1)}, f32[7,72,128]{2,1,0:T(8,128)}, u32[]{:S(2)}, u32[]{:S(2)}) collective-permute-start(f32[7,72,128]{2,1,0:T(8,128)S(1)} %get-tuple-element.105), channel_id=1, source_target_pairs={{0,1},{1,2},{2,3},{3,4},{4,5},{5,6},{6,7},{7,8},{8,9},{9,10},{10,1... | collective-permute-start | bytes 774152 | tf_op jit(solution)/shard_map/cond/branch_1_fun/ppermute | solution.py:530
  37.1 5.9 %collective-permute-start.34 = (f32[7,72,128]{2,1,0:T(8,128)S(1)}, f32[7,72,128]{2,1,0:T(8,128)}, u32[]{:S(2)}, u32[]{:S(2)}) collective-permute-start(f32[7,72,128]{2,1,0:T(8,128)S(1)} %get-tuple-element.106), channel_id=1, source_target_pairs={{0,63},{1,0},{2,1},{3,2},{4,3},{5,4},{6,5},{7,6},{8,7},{9,8},{10,9... | collective-permute-start | bytes 774152 | tf_op jit(solution)/shard_map/cond/branch_1_fun/ppermute | solution.py:530
  45.8 12.6 %all-to-all-start.1 = ((f32[4,7,48,128]{3,2,1,0:T(8,128)}), f32[4,7,48,128]{3,2,1,0:T(8,128)S(1)}, u32[]{:S(2)}, u32[]{:S(2)}) async-start(f32[4,7,48,128]{3,2,1,0:T(8,128)} %select.17), calls=%async_computation.1 | async-start | bytes 1376256 | tf_op jit(solution)/shard_map/all_to_all | solution.py:551
  50.0 3.7 %collective-permute-start.37 = (f32[7,8,128]{2,1,0:T(8,128)S(1)}, f32[7,8,128]{2,1,0:T(8,128)S(1)}, u32[]{:S(2)}, u32[]{:S(2)}) collective-permute-start(f32[7,8,128]{2,1,0:T(8,128)S(1)} %get-tuple-element.107), channel_id=1, source_target_pairs={{0,63},{1,0},{2,1},{3,2},{4,3},{5,4},{6,5},{7,6},{8,7},{9,8},{10,9... | collective-permute-start | bytes 86024 | tf_op jit(solution)/shard_map/ppermute | solution.py:530
  50.1 3.6 %collective-permute-start.36 = (f32[7,8,128]{2,1,0:T(8,128)S(1)}, f32[7,8,128]{2,1,0:T(8,128)S(1)}, u32[]{:S(2)}, u32[]{:S(2)}) collective-permute-start(f32[7,8,128]{2,1,0:T(8,128)S(1)} %get-tuple-element.108), channel_id=1, source_target_pairs={{0,1},{1,2},{2,3},{3,4},{4,5},{5,6},{6,7},{7,8},{8,9},{9,10},{10,1... | collective-permute-start | bytes 86024 | tf_op jit(solution)/shard_map/ppermute | solution.py:530

commit v4 on v3

--- a/solution.py
+++ b/solution.py
@@ -255,7 +255,22 @@
     return finish_with
 
 
-def gram_row(lefts, rights, pairs, exact, highs, lows, out):
+def pack_own(sources, packed):
+    lane = lax.broadcasted_iota(jnp.int32, (8, 128), 1)
+
+    def step(c, _):
+        for k, source in enumerate(sources):
+            out = pltpu.roll(source(4 * c), 128 - GHOST, 1)
+            for part in range(1, 4):
+                moved = pltpu.roll(source(4 * c + part), OWN * part - GHOST, 1)
+                out = jnp.where(lane >= OWN * part, moved, out)
+            packed[k, c] = out
+        return 0
+
+    lax.fori_loop(0, STEPS // 4, step, 0)
+
+
+def gram_row(lefts, rights, pairs, exact, columns, highs, lows, out):
     highs[...] = jnp.zeros(highs.shape, F32)
     lows[...] = jnp.zeros(lows.shape, F32)
     start = 0
@@ -282,7 +297,7 @@
             return tuple(out)
 
         zero = jnp.zeros((8, 128), F32)
-        sums = lax.fori_loop(0, STEPS, add, tuple((zero, zero) for _ in part), unroll=1 if exact else 2)
+        sums = lax.fori_loop(0, STEPS // 4 if exact else STEPS, add, tuple((zero, zero) for _ in part), unroll=1 if exact else 2)
         for (s, e), (_, _, lanes) in zip(sums, part):
             for lane in lanes:
                 highs[pl.ds(lane, 8, stride=128), :] = s
@@ -292,7 +307,7 @@
         s, err = two_sum(s, highs[128 * k : 128 * k + 128])
         e = e + (err + lows[128 * k : 128 * k + 128])
     s, e = s.T, e.T
-    hi, lo = sum_rows(jnp.concatenate([s[GHOST : GHOST + OWN], e[GHOST : GHOST + OWN]], axis=0))
+    hi, lo = sum_rows(jnp.concatenate([s[columns], e[columns]], axis=0))
     row = lax.broadcasted_iota(jnp.int32, (8, 128), 0)
     both = jnp.where((row & 1) == 0, jnp.broadcast_to(hi, (8, 128)), jnp.broadcast_to(lo, (8, 128)))
     out[...] = jnp.concatenate([both] * (out.shape[0] // 8), axis=0)
@@ -451,10 +466,10 @@
         operate(v_ref, i, w_ref, coef, fold, vp, ve, vw)
     lefts = [at(v_ref, i) for i in range(HALF)]
     rights = [at(w_ref, j) for j in range(HALF)] + [at(r0)]
-    gram_row(lefts, rights, gram_pairs(HALF), False, highs, lows, gram)
-
-
-def second_body(sums, coef, lines, below_mat, above_mat, fold, r0, v1, w1, r_ref, y_out, v_ref, w_ref, gram, y_buf, g_buf, vp, ve, vw, highs, lows):
+    gram_row(lefts, rights, gram_pairs(HALF), False, slice(GHOST, GHOST + OWN), highs, lows, gram)
+
+
+def second_body(sums, coef, lines, below_mat, above_mat, fold, r0, v1, w1, r_ref, y_out, v_ref, w_ref, gram, packed, y_buf, g_buf, vp, ve, vw, highs, lows):
     y, ratio = small_solve(*sum_rows(sums[...]), HALF)
     y_out[...] = y
     bound = ratio * (2.0 / SCALE)
@@ -480,9 +495,11 @@
             value = lambda t0, g, i=i: 2.0 * (v_ref[i - 1, pl.ds(t0, 8)] - step * g) - v_ref[i - 2, pl.ds(t0, 8)]
         line_solve(load, lines, below_mat, above_mat, y_buf, g_buf, finish_with(i, vp, ve, vw)(value))
         operate(v_ref, i, w_ref, coef, fold, vp, ve, vw)
-    lefts = [at(ref, i) for ref in (v1, v_ref) for i in range(HALF)]
-    rights = [at(ref, j) for ref in (w1, w_ref) for j in range(HALF)] + [at(r_ref)]
-    gram_row(lefts, rights, gram_pairs(TOTAL), True, highs, lows, gram)
+    vectors = [at(ref, i) for ref in (v1, v_ref, w1, w_ref) for i in range(HALF)] + [at(r_ref)]
+    pack_own(vectors, packed)
+    lefts = [at(packed, i) for i in range(TOTAL)]
+    rights = [at(packed, TOTAL + j) for j in range(TOTAL + 1)]
+    gram_row(lefts, rights, gram_pairs(TOTAL), True, slice(0, 128), highs, lows, gram)
 
 
 def last_body(sums, y1, r_ref, v1, w1, v2, w2, out, x_rows, r_rows):
@@ -603,7 +620,7 @@
             shape(HALF, *FIELD),
             shape(512, 128),
         ),
-        scratch_shapes=SCRATCH,
+        scratch_shapes=[vmem(2 * TOTAL + 1, STEPS // 4, 8, 128), *SCRATCH],
         name="phase_two",
         compiler_params=params(),
     )(sums, coef, lines, below_mat, above_mat, fold, r0, v1, w1)

time: 154 us -> 150 us (0.974)
  Pallas kernels: 33.7 us -> 29.7 us
    pallas_call x1, Pallas kernels: 13.2 us -> 9.31 us  [shards(): pl.pallas_call(second_body, out_shape=(shape(*FIELD), shape(8, 128), shap...]
where the time goes in v4:
time: 150 us; the launch traced here: 149 us
  blocking collectives  65.3 us (44%)
  waiting for transfers between devices  31.6 us (21%)
  Pallas kernels  29.7 us (20%)
  starting transfers between devices  19.1 us (13%)
  local copies, waits for them, and re-layouts  2.13 us (1%)
    all_to_all x2, blocking collectives, all_sums(): lax.all_to_all(gram, ('lat', *LON), split_axis=0, concat_axis=0, tiled=True)  45.6 us
    ppermute x1, waiting for transfers between devices, branch(): lax.ppermute(b, LON, [(d, (2 * q - d) % 64) for d in range(64)])  20.2 us
    all_to_all x2, blocking collectives, swap_lat(): lax.all_to_all(pieces, 'lat', split_axis=0, concat_axis=0, tiled=True)  19.7 us
    pallas_call x1, Pallas kernels, shards(): pl.pallas_call(first_body, out_shape=(shape(9, *FIELD), shape(6, STEPS +...  12.6 us
    ppermute x1, starting transfers between devices, branch(): lax.ppermute(b, LON, [(d, (2 * q - d) % 64) for d in range(64)])  10.8 us
    pallas_call x1, Pallas kernels, shards(): pl.pallas_call(second_body, out_shape=(shape(*FIELD), shape(8, 128), shap...  9.31 us
    ppermute x4, waiting for transfers between devices, ring(): return lax.ppermute(block, LON, [(d, (d + step) % 64) for d in range(64)])  6.68 us
    all_to_all x1, waiting for transfers between devices, swap_lat(): lax.all_to_all(pieces, 'lat', split_axis=0, concat_axis=0, tiled=True)  4.72 us
  transfers between devices with their start and end apart: 6, of which 5 were waited for; matrix products, arithmetic and copies ran while one was open for 1% of the time, Pallas kernels for 0%

profile of v4, /device:TPU:1, one launch (start us, length us, event | category | flops | bytes accessed | tf_op | source)
XLA Modules:
  0.0 149.3 jit_solution(14537388620892874405)
XLA Ops:
  1.4 1.2 pack.1.packed
  2.6 31.0 %conditional.2 = (f32[7,128,128]{2,1,0:T(8,128)}) conditional(s32[]{:T(128)} %clamp.3, f32[7,128,128]{2,1,0:T(8,128)S(1)} %pack.1.packed, f32[7,128,128]{2,1,0:T(8,128)S(1)} %pack.1.packed, f32[7,128,128]{2,1,0:T(8,128)S(1)} %pack.1.packed, f32[7,128,128]{2,1,0:T(8,128)S(1)} %pack.1.packed, ...), branch_computations={%region_0.1_spmd, %region_1.2_spmd, %region_2.3_spmd, %region_3.4_... | conditional | bytes 1835056 | solution.py:554
  2.6 10.8 %collective-permute-start.24 = (f32[7,128,128]{2,1,0:T(8,128)S(1)}, f32[7,128,128]{2,1,0:T(8,128)}, u32[]{:S(2)}, u32[]{:S(2)}) collective-permute-start(f32[7,128,128]{2,1,0:T(8,128)S(1)} %param.24), channel_id=1, source_target_pairs={{0,48},{1,47},{2,46},{3,45},{4,44},{5,43},{6,42},{7,41},{8,40},{9,... | collective-permute-start | bytes 1376264 | tf_op jit(solution)/shard_map/cond/branch_24_fun/ppermute | solution.py:552
  13.4 20.2 %collective-permute-done.24 = f32[7,128,128]{2,1,0:T(8,128)} collective-permute-done((f32[7,128,128]{2,1,0:T(8,128)S(1)}, f32[7,128,128]{2,1,0:T(8,128)}, u32[]{:S(2)}, u32[]{:S(2)}) %collective-permute-start.24) | collective-permute-done | bytes 458784 | tf_op jit(solution)/shard_map/cond/branch_24_fun/ppermute | solution.py:552
  33.6 9.3 %conditional.3 = (f32[7,72,128]{2,1,0:T(8,128)}, f32[7,128,128]{2,1,0:T(8,128)S(1)}, f32[7,72,128]{2,1,0:T(8,128)}) conditional(s32[]{:T(128)} %convert_element_type.3, f32[7,128,128]{2,1,0:T(8,128)} %get-tuple-element.115, f32[7,128,128]{2,1,0:T(8,128)} %get-tuple-element.115), branch_computations={%region_32.33_spmd, %region_33.34_spmd} | conditional | bytes 4014184 | solution.py:564
  33.6 1.1 fusion.1
  34.7 2.4 %collective-permute-start.35 = (f32[7,72,128]{2,1,0:T(8,128)S(1)}, f32[7,72,128]{2,1,0:T(8,128)}, u32[]{:S(2)}, u32[]{:S(2)}) collective-permute-start(f32[7,72,128]{2,1,0:T(8,128)S(1)} %get-tuple-element.105), channel_id=1, source_target_pairs={{0,1},{1,2},{2,3},{3,4},{4,5},{5,6},{6,7},{7,8},{8,9},{9,10},{10,1... | collective-permute-start | bytes 774152 | tf_op jit(solution)/shard_map/cond/branch_1_fun/ppermute | solution.py:547
  37.1 1.0 copy.46
  38.1 2.3 %collective-permute-done.35 = f32[7,72,128]{2,1,0:T(8,128)} collective-permute-done((f32[7,72,128]{2,1,0:T(8,128)S(1)}, f32[7,72,128]{2,1,0:T(8,128)}, u32[]{:S(2)}, u32[]{:S(2)}) %collective-permute-start.35) | collective-permute-done | bytes 258080 | tf_op jit(solution)/shard_map/cond/branch_1_fun/ppermute | solution.py:547
  40.3 2.6 %collective-permute-done.34 = f32[7,72,128]{2,1,0:T(8,128)} collective-permute-done((f32[7,72,128]{2,1,0:T(8,128)S(1)}, f32[7,72,128]{2,1,0:T(8,128)}, u32[]{:S(2)}, u32[]{:S(2)}) %collective-permute-start.34) | collective-permute-done | bytes 258080 | tf_op jit(solution)/shard_map/cond/branch_1_fun/ppermute | solution.py:547
  42.9 2.9 %select.17 = f32[4,7,48,128]{3,2,1,0:T(8,128)} custom-call(s32[1]{0:T(128)} %bitcast.1.shift, f32[7,72,128]{2,1,0:T(8,128)} %get-tuple-element.86.low, f32[7,128,128]{2,1,0:T(8,128)S(1)} %get-tuple-element.87.main, f32[7,72,128]{2,1,0:T(8,128)} %get-tuple-element.88.high), custom_call_target="tpu_custom_call" | custom-call | tf_op jit(solution)/shard_map/select/pallas_call | solution.py:588
  45.8 4.2 %all-to-all-start.1 = ((f32[4,7,48,128]{3,2,1,0:T(8,128)}), f32[4,7,48,128]{3,2,1,0:T(8,128)S(1)}, u32[]{:S(2)}, u32[]{:S(2)}) async-start(f32[4,7,48,128]{3,2,1,0:T(8,128)} %select.17), calls=%async_computation.1 | async-start | bytes 1376256 | tf_op jit(solution)/shard_map/all_to_all | solution.py:568
  50.0 0.1 collective-permute-start.37
  50.1 1.7 %collective-permute-start.36 = (f32[7,8,128]{2,1,0:T(8,128)S(1)}, f32[7,8,128]{2,1,0:T(8,128)S(1)}, u32[]{:S(2)}, u32[]{:S(2)}) collective-permute-start(f32[7,8,128]{2,1,0:T(8,128)S(1)} %get-tuple-element.108), channel_id=1, source_target_pairs={{0,1},{1,2},{2,3},{3,4},{4,5},{5,6},{6,7},{7,8},{8,9},{9,10},{10,1... | collective-permute-start | bytes 86024 | tf_op jit(solution)/shard_map/ppermute | solution.py:547
  51.8 1.8 %collective-permute-done.37.after = f32[7,8,128]{2,1,0:T(8,128)S(1)} collective-permute-done((f32[7,8,128]{2,1,0:T(8,128)S(1)}, f32[7,8,128]{2,1,0:T(8,128)S(1)}, u32[]{:S(2)}, u32[]{:S(2)}) %collective-permute-start.37) | collective-permute-done | bytes 28704 | tf_op jit(solution)/shard_map/ppermute | solution.py:547
  53.7 4.7 %all-to-all-done.1.facing = f32[4,7,48,128]{3,2,1,0:T(8,128)S(1)} async-done(((f32[4,7,48,128]{3,2,1,0:T(8,128)}), f32[4,7,48,128]{3,2,1,0:T(8,128)S(1)}, u32[]{:S(2)}, u32[]{:S(2)}) %all-to-all-start.1) | async-done | bytes 688160 | tf_op jit(solution)/shard_map/all_to_all | solution.py:568
  58.4 11.8 %all_to_all.37.own = f32[4,7,48,128]{3,2,1,0:T(8,128)S(1)} all-to-all(f32[4,7,48,128]{3,2,1,0:T(8,128)S(1)} %window.1), channel_id=1, replica_groups=mesh['lat'=4,'x'=4,'z'=8,'core'=2] {'lat'}, dimensions={0} | all-to-all | bytes 1376256 | tf_op jit(solution)/shard_map/all_to_all | solution.py:568
  70.2 12.6 %phase_one.1 = (f32[9,64,8,128]{3,2,1,0:T(8,128)S(1)}, f32[6,72,8,128]{3,2,1,0:T(8,128)S(1)}, f32[16,8,128]{2,1,0:T(8,128)S(1)}, f32[16,8,128]{2,1,0:T(8,128)S(1...) custom-call(f32[4,7,48,128]{3,2,1,0:T(8,128)S(1)} %all_to_all.37.own, ...), custom_call_target="tpu_custom_call" | custom-call | tf_op jit(solution)/shard_map/phase_one/pallas_call | solution.py:596
  82.8 24.4 %all_to_all.38 = f32[256,2,128]{2,1,0:T(2,128)S(1)} all-to-all(f32[256,2,128]{2,1,0:T(2,128)S(1)} %bitcast.10), channel_id=1, replica_groups=mesh['lat'=4,'x'=4,'z'=8,'core'=2] {'lat','x','z','core'}, dimensions={0} | all-to-all | bytes 524288 | tf_op jit(solution)/shard_map/all_to_all | solution.py:543
  107.2 9.3 %phase_two.1 = (f32[64,8,128]{2,1,0:T(8,128)S(1)}, f32[8,128]{1,0:T(8,128)S(1)}, f32[4,64,8,128]{3,2,1,0:T(8,128)S(1)}, f32[4,64,8,128]{3,2,1,0:T(8,128)S(1)}, f32[512,128]{1,0:T(8,128)S(1)}) custom-call(f32[512,128]{1,0:T(8,128)S(1)} %bitcast.7, f32[9,64,8,128]{3,2,1,0:T(8,128)S(1)} %get-tuple-element.90.coef, ...), custom_call_target="tpu_custom_call" | custom-call | tf_op jit(solution)/shard_map/phase_two/pallas_call | solution.py:614
  116.5 21.2 %all_to_all.39 = f32[256,2,128]{2,1,0:T(2,128)S(1)} all-to-all(f32[256,2,128]{2,1,0:T(2,128)S(1)} %bitcast.9), channel_id=1, replica_groups=mesh['lat'=4,'x'=4,'z'=8,'core'=2] {'lat','x','z','core'}, dimensions={0} | all-to-all | bytes 524288 | tf_op jit(solution)/shard_map/all_to_all | solution.py:543
  137.7 2.0 %combine.1 = f32[4,2,32,128]{3,2,1,0:T(8,128)S(1)} custom-call(f32[512,128]{1,0:T(8,128)S(1)} %bitcast.8, f32[8,128]{1,0:T(8,128)S(1)} %get-tuple-element.99.y1, f32[64,8,128]{2,1,0:T(8,128)S(1)} %get-tuple-element.100.r_ref, f32[4,64,8,128]{3,2,1,0:T(8,128)S(1)} %get-tuple-element.96.v1, f32[4,64,8,128]{3,2,1,0:T(8,128)S(1)} %get-tuple-element.97.w1, ...), custom_call_target="tpu_custom_call" | custom-call | tf_op jit(solution)/shard_map/combine/pallas_call | solution.py:628
  139.8 7.9 %all_to_all.40.recv = f32[4,2,32,128]{3,2,1,0:T(8,128)} all-to-all(f32[4,2,32,128]{3,2,1,0:T(8,128)S(1)} %combine.1), channel_id=1, replica_groups=mesh['lat'=4,'x'=4,'z'=8,'core'=2] {'lat'}, dimensions={0} | all-to-all | bytes 262144 | tf_op jit(solution)/shard_map/all_to_all | solution.py:568
  147.6 1.7 %unpack.1 = (f32[128,128]{1,0:T(8,128)}, f32[128,128]{1,0:T(8,128)}) custom-call(f32[4,2,32,128]{3,2,1,0:T(8,128)} %all_to_all.40.recv), custom_call_target="tpu_custom_call" | custom-call | tf_op jit(solution)/shard_map/unpack/pallas_call | solution.py:636
  (4 shorter events, 0.1 us)
Async XLA Ops:
  2.6 30.9 %collective-permute-start.24 = (f32[7,128,128]{2,1,0:T(8,128)S(1)}, f32[7,128,128]{2,1,0:T(8,128)}, u32[]{:S(2)}, u32[]{:S(2)}) collective-permute-start(f32[7,128,128]{2,1,0:T(8,128)S(1)} %param.24), channel_id=1, source_target_pairs={{0,48},{1,47},{2,46},{3,45},{4,44},{5,43},{6,42},{7,41},{8,40},{9,... | collective-permute-start | bytes 1376264 | tf_op jit(solution)/shard_map/cond/branch_24_fun/ppermute | solution.py:552
  34.7 5.7 %collective-permute-start.35 = (f32[7,72,128]{2,1,0:T(8,128)S(1)}, f32[7,72,128]{2,1,0:T(8,128)}, u32[]{:S(2)}, u32[]{:S(2)}) collective-permute-start(f32[7,72,128]{2,1,0:T(8,128)S(1)} %get-tuple-element.105), channel_id=1, source_target_pairs={{0,1},{1,2},{2,3},{3,4},{4,5},{5,6},{6,7},{7,8},{8,9},{9,10},{10,1... | collective-permute-start | bytes 774152 | tf_op jit(solution)/shard_map/cond/branch_1_fun/ppermute | solution.py:547
  37.1 5.9 %collective-permute-start.34 = (f32[7,72,128]{2,1,0:T(8,128)S(1)}, f32[7,72,128]{2,1,0:T(8,128)}, u32[]{:S(2)}, u32[]{:S(2)}) collective-permute-start(f32[7,72,128]{2,1,0:T(8,128)S(1)} %get-tuple-element.106), channel_id=1, source_target_pairs={{0,63},{1,0},{2,1},{3,2},{4,3},{5,4},{6,5},{7,6},{8,7},{9,8},{10,9... | collective-permute-start | bytes 774152 | tf_op jit(solution)/shard_map/cond/branch_1_fun/ppermute | solution.py:547
  45.8 12.6 %all-to-all-start.1 = ((f32[4,7,48,128]{3,2,1,0:T(8,128)}), f32[4,7,48,128]{3,2,1,0:T(8,128)S(1)}, u32[]{:S(2)}, u32[]{:S(2)}) async-start(f32[4,7,48,128]{3,2,1,0:T(8,128)} %select.17), calls=%async_computation.1 | async-start | bytes 1376256 | tf_op jit(solution)/shard_map/all_to_all | solution.py:568
  50.0 3.7 %collective-permute-start.37 = (f32[7,8,128]{2,1,0:T(8,128)S(1)}, f32[7,8,128]{2,1,0:T(8,128)S(1)}, u32[]{:S(2)}, u32[]{:S(2)}) collective-permute-start(f32[7,8,128]{2,1,0:T(8,128)S(1)} %get-tuple-element.107), channel_id=1, source_target_pairs={{0,63},{1,0},{2,1},{3,2},{4,3},{5,4},{6,5},{7,6},{8,7},{9,8},{10,9... | collective-permute-start | bytes 86024 | tf_op jit(solution)/shard_map/ppermute | solution.py:547
  50.1 3.6 %collective-permute-start.36 = (f32[7,8,128]{2,1,0:T(8,128)S(1)}, f32[7,8,128]{2,1,0:T(8,128)S(1)}, u32[]{:S(2)}, u32[]{:S(2)}) collective-permute-start(f32[7,8,128]{2,1,0:T(8,128)S(1)} %get-tuple-element.108), channel_id=1, source_target_pairs={{0,1},{1,2},{2,3},{3,4},{4,5},{5,6},{6,7},{7,8},{8,9},{9,10},{10,1... | collective-permute-start | bytes 86024 | tf_op jit(solution)/shard_map/ppermute | solution.py:547

commit v5 on v4

--- a/solution.py
+++ b/solution.py
@@ -309,7 +309,9 @@
     s, e = s.T, e.T
     hi, lo = sum_rows(jnp.concatenate([s[columns], e[columns]], axis=0))
     row = lax.broadcasted_iota(jnp.int32, (8, 128), 0)
-    both = jnp.where((row & 1) == 0, jnp.broadcast_to(hi, (8, 128)), jnp.broadcast_to(lo, (8, 128)))
+    both = jnp.broadcast_to(hi, (8, 128))
+    if exact:
+        both = jnp.where((row & 1) == 0, both, jnp.broadcast_to(lo, (8, 128)))
     out[...] = jnp.concatenate([both] * (out.shape[0] // 8), axis=0)
 
 
@@ -382,9 +384,10 @@
         more, err = two_sum(pivot, -north)
         more = more + err
         y_buf[t] = more - ratio * beyond
-        guess = north / pivot
+        inverse = 1.0 / pivot
+        guess = north * inverse
         prod, err = two_prod(guess, pivot)
-        return guess + ((north - prod) - err) / pivot, more
+        return guess + ((north - prod) - err) * inverse, more
 
     ends = lax.fori_loop(0, STEPS, eliminate, (zero, zero), unroll=2)
     lax.fori_loop(0, STEPS, eliminate, tuple(row_before(v) for v in ends), unroll=2)
@@ -604,7 +607,7 @@
             shape(*FIELD),
             shape(HALF, *FIELD),
             shape(HALF, *FIELD),
-            shape(512, 128),
+            shape(256, 128),
         ),
         scratch_shapes=[vmem(7, 512, 128), vmem(7, STEPS + 2, 8, 128), *SCRATCH],
         name="phase_one",

time: 150 us -> 147 us (0.980)
  blocking collectives: 65.3 us -> 62.6 us
    all_to_all x2, blocking collectives: 45.6 us -> 43 us  [all_sums(): lax.all_to_all(gram, ('lat', *LON), split_axis=0, concat_axis=0, tiled=True)]
where the time goes in v5:
time: 147 us
  blocking collectives  62.6 us (43%)
  waiting for transfers between devices  31.6 us (21%)
  Pallas kernels  29.7 us (20%)
  starting transfers between devices  19.1 us (13%)
  local copies, waits for them, and re-layouts  2.13 us (1%)
    all_to_all x2, blocking collectives, all_sums(): lax.all_to_all(gram, ('lat', *LON), split_axis=0, concat_axis=0, tiled=True)  43 us
    ppermute x1, waiting for transfers between devices, branch(): lax.ppermute(b, LON, [(d, (2 * q - d) % 64) for d in range(64)])  20.2 us
    all_to_all x2, blocking collectives, swap_lat(): lax.all_to_all(pieces, 'lat', split_axis=0, concat_axis=0, tiled=True)  19.7 us
    pallas_call x1, Pallas kernels, shards(): pl.pallas_call(first_body, out_shape=(shape(9, *FIELD), shape(6, STEPS +...  12.6 us
    ppermute x1, starting transfers between devices, branch(): lax.ppermute(b, LON, [(d, (2 * q - d) % 64) for d in range(64)])  10.8 us
    pallas_call x1, Pallas kernels, shards(): pl.pallas_call(second_body, out_shape=(shape(*FIELD), shape(8, 128), shap...  9.28 us
    ppermute x4, waiting for transfers between devices, ring(): return lax.ppermute(block, LON, [(d, (d + step) % 64) for d in range(64)])  6.68 us
    all_to_all x1, waiting for transfers between devices, swap_lat(): lax.all_to_all(pieces, 'lat', split_axis=0, concat_axis=0, tiled=True)  4.72 us
  transfers between devices with their start and end apart: 6, of which 5 were waited for; matrix products, arithmetic and copies ran while one was open for 1% of the time, Pallas kernels for 0%

profile of v5, /device:TPU:1, one launch (start us, length us, event | category | flops | bytes accessed | tf_op | source)
XLA Modules:
  0.0 146.6 jit_solution(12784385697062017044)
XLA Ops:
  1.4 1.2 pack.1.packed
  2.6 31.0 %conditional.2 = (f32[7,128,128]{2,1,0:T(8,128)}) conditional(s32[]{:T(128)} %clamp.3, f32[7,128,128]{2,1,0:T(8,128)S(1)} %pack.1.packed, f32[7,128,128]{2,1,0:T(8,128)S(1)} %pack.1.packed, f32[7,128,128]{2,1,0:T(8,128)S(1)} %pack.1.packed, f32[7,128,128]{2,1,0:T(8,128)S(1)} %pack.1.packed, ...), branch_computations={%region_0.1_spmd, %region_1.2_spmd, %region_2.3_spmd, %region_3.4_... | conditional | bytes 1835056 | solution.py:557
  2.6 10.8 %collective-permute-start.24 = (f32[7,128,128]{2,1,0:T(8,128)S(1)}, f32[7,128,128]{2,1,0:T(8,128)}, u32[]{:S(2)}, u32[]{:S(2)}) collective-permute-start(f32[7,128,128]{2,1,0:T(8,128)S(1)} %param.24), channel_id=1, source_target_pairs={{0,48},{1,47},{2,46},{3,45},{4,44},{5,43},{6,42},{7,41},{8,40},{9,... | collective-permute-start | bytes 1376264 | tf_op jit(solution)/shard_map/cond/branch_24_fun/ppermute | solution.py:555
  13.4 20.2 %collective-permute-done.24 = f32[7,128,128]{2,1,0:T(8,128)} collective-permute-done((f32[7,128,128]{2,1,0:T(8,128)S(1)}, f32[7,128,128]{2,1,0:T(8,128)}, u32[]{:S(2)}, u32[]{:S(2)}) %collective-permute-start.24) | collective-permute-done | bytes 458784 | tf_op jit(solution)/shard_map/cond/branch_24_fun/ppermute | solution.py:555
  33.6 9.3 %conditional.3 = (f32[7,72,128]{2,1,0:T(8,128)}, f32[7,128,128]{2,1,0:T(8,128)S(1)}, f32[7,72,128]{2,1,0:T(8,128)}) conditional(s32[]{:T(128)} %convert_element_type.3, f32[7,128,128]{2,1,0:T(8,128)} %get-tuple-element.115, f32[7,128,128]{2,1,0:T(8,128)} %get-tuple-element.115), branch_computations={%region_32.33_spmd, %region_33.34_spmd} | conditional | bytes 4014184 | solution.py:567
  33.6 1.1 fusion.1
  34.7 2.4 %collective-permute-start.35 = (f32[7,72,128]{2,1,0:T(8,128)S(1)}, f32[7,72,128]{2,1,0:T(8,128)}, u32[]{:S(2)}, u32[]{:S(2)}) collective-permute-start(f32[7,72,128]{2,1,0:T(8,128)S(1)} %get-tuple-element.105), channel_id=1, source_target_pairs={{0,1},{1,2},{2,3},{3,4},{4,5},{5,6},{6,7},{7,8},{8,9},{9,10},{10,1... | collective-permute-start | bytes 774152 | tf_op jit(solution)/shard_map/cond/branch_1_fun/ppermute | solution.py:550
  37.1 1.0 copy.47
  38.1 2.3 %collective-permute-done.35 = f32[7,72,128]{2,1,0:T(8,128)} collective-permute-done((f32[7,72,128]{2,1,0:T(8,128)S(1)}, f32[7,72,128]{2,1,0:T(8,128)}, u32[]{:S(2)}, u32[]{:S(2)}) %collective-permute-start.35) | collective-permute-done | bytes 258080 | tf_op jit(solution)/shard_map/cond/branch_1_fun/ppermute | solution.py:550
  40.3 2.6 %collective-permute-done.34 = f32[7,72,128]{2,1,0:T(8,128)} collective-permute-done((f32[7,72,128]{2,1,0:T(8,128)S(1)}, f32[7,72,128]{2,1,0:T(8,128)}, u32[]{:S(2)}, u32[]{:S(2)}) %collective-permute-start.34) | collective-permute-done | bytes 258080 | tf_op jit(solution)/shard_map/cond/branch_1_fun/ppermute | solution.py:550
  42.9 2.9 %select.17 = f32[4,7,48,128]{3,2,1,0:T(8,128)} custom-call(s32[1]{0:T(128)} %bitcast.1.shift, f32[7,72,128]{2,1,0:T(8,128)} %get-tuple-element.86.low, f32[7,128,128]{2,1,0:T(8,128)S(1)} %get-tuple-element.87.main, f32[7,72,128]{2,1,0:T(8,128)} %get-tuple-element.88.high), custom_call_target="tpu_custom_call" | custom-call | tf_op jit(solution)/shard_map/select/pallas_call | solution.py:591
  45.8 4.2 %all-to-all-start.1 = ((f32[4,7,48,128]{3,2,1,0:T(8,128)}), f32[4,7,48,128]{3,2,1,0:T(8,128)S(1)}, u32[]{:S(2)}, u32[]{:S(2)}) async-start(f32[4,7,48,128]{3,2,1,0:T(8,128)} %select.17), calls=%async_computation.1 | async-start | bytes 1376256 | tf_op jit(solution)/shard_map/all_to_all | solution.py:571
  50.0 0.1 collective-permute-start.37
  50.1 1.7 %collective-permute-start.36 = (f32[7,8,128]{2,1,0:T(8,128)S(1)}, f32[7,8,128]{2,1,0:T(8,128)S(1)}, u32[]{:S(2)}, u32[]{:S(2)}) collective-permute-start(f32[7,8,128]{2,1,0:T(8,128)S(1)} %get-tuple-element.108), channel_id=1, source_target_pairs={{0,1},{1,2},{2,3},{3,4},{4,5},{5,6},{6,7},{7,8},{8,9},{9,10},{10,1... | collective-permute-start | bytes 86024 | tf_op jit(solution)/shard_map/ppermute | solution.py:550
  51.8 1.8 %collective-permute-done.37.after = f32[7,8,128]{2,1,0:T(8,128)S(1)} collective-permute-done((f32[7,8,128]{2,1,0:T(8,128)S(1)}, f32[7,8,128]{2,1,0:T(8,128)S(1)}, u32[]{:S(2)}, u32[]{:S(2)}) %collective-permute-start.37) | collective-permute-done | bytes 28704 | tf_op jit(solution)/shard_map/ppermute | solution.py:550
  53.7 4.7 %all-to-all-done.1.facing = f32[4,7,48,128]{3,2,1,0:T(8,128)S(1)} async-done(((f32[4,7,48,128]{3,2,1,0:T(8,128)}), f32[4,7,48,128]{3,2,1,0:T(8,128)S(1)}, u32[]{:S(2)}, u32[]{:S(2)}) %all-to-all-start.1) | async-done | bytes 688160 | tf_op jit(solution)/shard_map/all_to_all | solution.py:571
  58.4 11.8 %all_to_all.37.own = f32[4,7,48,128]{3,2,1,0:T(8,128)S(1)} all-to-all(f32[4,7,48,128]{3,2,1,0:T(8,128)S(1)} %window.1), channel_id=1, replica_groups=mesh['lat'=4,'x'=4,'z'=8,'core'=2] {'lat'}, dimensions={0} | all-to-all | bytes 1376256 | tf_op jit(solution)/shard_map/all_to_all | solution.py:571
  70.2 12.6 %phase_one.1 = (f32[9,64,8,128]{3,2,1,0:T(8,128)S(1)}, f32[6,72,8,128]{3,2,1,0:T(8,128)S(1)}, f32[16,8,128]{2,1,0:T(8,128)S(1)}, f32[16,8,128]{2,1,0:T(8,128)S(1...) custom-call(f32[4,7,48,128]{3,2,1,0:T(8,128)S(1)} %all_to_all.37.own, ...), custom_call_target="tpu_custom_call" | custom-call | tf_op jit(solution)/shard_map/phase_one/pallas_call | solution.py:599
  82.8 21.3 %all_to_all.38 = f32[256,1,128]{2,1,0:T(1,128)S(1)} all-to-all(f32[256,1,128]{2,1,0:T(1,128)S(1)} %bitcast.12), channel_id=1, replica_groups=mesh['lat'=4,'x'=4,'z'=8,'core'=2] {'lat','x','z','core'}, dimensions={0} | all-to-all | bytes 262144 | tf_op jit(solution)/shard_map/all_to_all | solution.py:546
  104.2 9.3 %phase_two.1 = (f32[64,8,128]{2,1,0:T(8,128)S(1)}, f32[8,128]{1,0:T(8,128)S(1)}, f32[4,64,8,128]{3,2,1,0:T(8,128)S(1)}, f32[4,64,8,128]{3,2,1,0:T(8,128)S(1)}, f32[512,128]{1,0:T(8,128)S(1)}) custom-call(f32[256,128]{1,0:T(8,128)S(1)} %bitcast.10, f32[9,64,8,128]{3,2,1,0:T(8,128)S(1)} %get-tuple-element.90.coef, ...), custom_call_target="tpu_custom_call" | custom-call | tf_op jit(solution)/shard_map/phase_two/pallas_call | solution.py:617
  113.4 21.6 %all_to_all.39 = f32[256,2,128]{2,1,0:T(2,128)S(1)} all-to-all(f32[256,2,128]{2,1,0:T(2,128)S(1)} %bitcast.11), channel_id=1, replica_groups=mesh['lat'=4,'x'=4,'z'=8,'core'=2] {'lat','x','z','core'}, dimensions={0} | all-to-all | bytes 524288 | tf_op jit(solution)/shard_map/all_to_all | solution.py:546
  135.1 2.0 %combine.1 = f32[4,2,32,128]{3,2,1,0:T(8,128)S(1)} custom-call(f32[512,128]{1,0:T(8,128)S(1)} %bitcast.9, f32[8,128]{1,0:T(8,128)S(1)} %get-tuple-element.99.y1, f32[64,8,128]{2,1,0:T(8,128)S(1)} %get-tuple-element.100.r_ref, f32[4,64,8,128]{3,2,1,0:T(8,128)S(1)} %get-tuple-element.96.v1, f32[4,64,8,128]{3,2,1,0:T(8,128)S(1)} %get-tuple-element.97.w1, ...), custom_call_target="tpu_custom_call" | custom-call | tf_op jit(solution)/shard_map/combine/pallas_call | solution.py:631
  137.1 7.9 %all_to_all.40.recv = f32[4,2,32,128]{3,2,1,0:T(8,128)} all-to-all(f32[4,2,32,128]{3,2,1,0:T(8,128)S(1)} %combine.1), channel_id=1, replica_groups=mesh['lat'=4,'x'=4,'z'=8,'core'=2] {'lat'}, dimensions={0} | all-to-all | bytes 262144 | tf_op jit(solution)/shard_map/all_to_all | solution.py:571
  145.0 1.7 %unpack.1 = (f32[128,128]{1,0:T(8,128)}, f32[128,128]{1,0:T(8,128)}) custom-call(f32[4,2,32,128]{3,2,1,0:T(8,128)} %all_to_all.40.recv), custom_call_target="tpu_custom_call" | custom-call | tf_op jit(solution)/shard_map/unpack/pallas_call | solution.py:639
  (4 shorter events, 0.1 us)
Async XLA Ops:
  2.6 30.9 %collective-permute-start.24 = (f32[7,128,128]{2,1,0:T(8,128)S(1)}, f32[7,128,128]{2,1,0:T(8,128)}, u32[]{:S(2)}, u32[]{:S(2)}) collective-permute-start(f32[7,128,128]{2,1,0:T(8,128)S(1)} %param.24), channel_id=1, source_target_pairs={{0,48},{1,47},{2,46},{3,45},{4,44},{5,43},{6,42},{7,41},{8,40},{9,... | collective-permute-start | bytes 1376264 | tf_op jit(solution)/shard_map/cond/branch_24_fun/ppermute | solution.py:555
  34.7 5.7 %collective-permute-start.35 = (f32[7,72,128]{2,1,0:T(8,128)S(1)}, f32[7,72,128]{2,1,0:T(8,128)}, u32[]{:S(2)}, u32[]{:S(2)}) collective-permute-start(f32[7,72,128]{2,1,0:T(8,128)S(1)} %get-tuple-element.105), channel_id=1, source_target_pairs={{0,1},{1,2},{2,3},{3,4},{4,5},{5,6},{6,7},{7,8},{8,9},{9,10},{10,1... | collective-permute-start | bytes 774152 | tf_op jit(solution)/shard_map/cond/branch_1_fun/ppermute | solution.py:550
  37.1 5.9 %collective-permute-start.34 = (f32[7,72,128]{2,1,0:T(8,128)S(1)}, f32[7,72,128]{2,1,0:T(8,128)}, u32[]{:S(2)}, u32[]{:S(2)}) collective-permute-start(f32[7,72,128]{2,1,0:T(8,128)S(1)} %get-tuple-element.106), channel_id=1, source_target_pairs={{0,63},{1,0},{2,1},{3,2},{4,3},{5,4},{6,5},{7,6},{8,7},{9,8},{10,9... | collective-permute-start | bytes 774152 | tf_op jit(solution)/shard_map/cond/branch_1_fun/ppermute | solution.py:550
  45.8 12.6 %all-to-all-start.1 = ((f32[4,7,48,128]{3,2,1,0:T(8,128)}), f32[4,7,48,128]{3,2,1,0:T(8,128)S(1)}, u32[]{:S(2)}, u32[]{:S(2)}) async-start(f32[4,7,48,128]{3,2,1,0:T(8,128)} %select.17), calls=%async_computation.1 | async-start | bytes 1376256 | tf_op jit(solution)/shard_map/all_to_all | solution.py:571
  50.0 3.7 %collective-permute-start.37 = (f32[7,8,128]{2,1,0:T(8,128)S(1)}, f32[7,8,128]{2,1,0:T(8,128)S(1)}, u32[]{:S(2)}, u32[]{:S(2)}) collective-permute-start(f32[7,8,128]{2,1,0:T(8,128)S(1)} %get-tuple-element.107), channel_id=1, source_target_pairs={{0,63},{1,0},{2,1},{3,2},{4,3},{5,4},{6,5},{7,6},{8,7},{9,8},{10,9... | collective-permute-start | bytes 86024 | tf_op jit(solution)/shard_map/ppermute | solution.py:550
  50.1 3.6 %collective-permute-start.36 = (f32[7,8,128]{2,1,0:T(8,128)S(1)}, f32[7,8,128]{2,1,0:T(8,128)S(1)}, u32[]{:S(2)}, u32[]{:S(2)}) collective-permute-start(f32[7,8,128]{2,1,0:T(8,128)S(1)} %get-tuple-element.108), channel_id=1, source_target_pairs={{0,1},{1,2},{2,3},{3,4},{4,5},{5,6},{6,7},{7,8},{8,9},{9,10},{10,1... | collective-permute-start | bytes 86024 | tf_op jit(solution)/shard_map/ppermute | solution.py:550

commit v6 on v5

--- a/solution.py
+++ b/solution.py
@@ -17,6 +17,8 @@
 WIDE = OWN + 2 * GHOST
 PAD = COLS + 2 * GHOST
 STEPS = 64
+LINE = STEPS + 8
+SLAB = 128 + 8
 HALF = 4
 TOTAL = 2 * HALF
 SCALE = 1.0e-4
@@ -300,12 +302,12 @@
         sums = lax.fori_loop(0, STEPS // 4 if exact else STEPS, add, tuple((zero, zero) for _ in part), unroll=1 if exact else 2)
         for (s, e), (_, _, lanes) in zip(sums, part):
             for lane in lanes:
-                highs[pl.ds(lane, 8, stride=128), :] = s
-                lows[pl.ds(lane, 8, stride=128), :] = e
+                highs[pl.ds(lane, 8, stride=SLAB), :] = s
+                lows[pl.ds(lane, 8, stride=SLAB), :] = e
     s, e = highs[0:128], lows[0:128]
     for k in range(1, 8):
-        s, err = two_sum(s, highs[128 * k : 128 * k + 128])
-        e = e + (err + lows[128 * k : 128 * k + 128])
+        s, err = two_sum(s, highs[SLAB * k : SLAB * k + 128])
+        e = e + (err + lows[SLAB * k : SLAB * k + 128])
     s, e = s.T, e.T
     hi, lo = sum_rows(jnp.concatenate([s[columns], e[columns]], axis=0))
     row = lax.broadcasted_iota(jnp.int32, (8, 128), 0)
@@ -334,9 +336,12 @@
     for place in range(7):
         for source in range(4):
             full = jnp.concatenate([own[source, place], gap, facing[source, place], gap], axis=0)
-            raw[place, 128 * source : 128 * source + 128, :] = full.T
+            full = full.T
+            for part in range(2):
+                row = LINE * (2 * source + part)
+                raw[place, row : row + STEPS, :] = full[STEPS * part : STEPS * part + STEPS]
         for t in range(STEPS):
-            grid[place, t + 1] = raw[place, pl.ds(t, 8, stride=STEPS), :]
+            grid[place, t + 1] = raw[place, pl.ds(t, 8, stride=LINE), :]
     top_north = grid[3, STEPS]
     top_ocean = grid[6, STEPS]
     last = s_id == 7
@@ -380,7 +385,7 @@
     def eliminate(t, carry):
         ratio, beyond = carry
         north = coef[N, t]
-        pivot = vw[t] - coef[S, t] * ratio
+        pivot = vw[t] - jnp.maximum(coef[S, t] * ratio, 0.0)
         more, err = two_sum(pivot, -north)
         more = more + err
         y_buf[t] = more - ratio * beyond
@@ -518,11 +523,12 @@
         for i in range(HALF):
             x = x + v_weights[HALF + i] * v2[i, t]
             r = r - w_weights[HALF + i] * w2[i, t]
-        x_rows[pl.ds(t, 8, stride=STEPS), :] = x
-        r_rows[pl.ds(t, 8, stride=STEPS), :] = r
+        x_rows[pl.ds(t, 8, stride=LINE), :] = x
+        r_rows[pl.ds(t, 8, stride=LINE), :] = r
     for place, rows in enumerate((x_rows, r_rows)):
         for part in range(4):
-            out[part, place] = rows[128 * part : 128 * part + 128, :].T[GHOST : GHOST + OWN, :]
+            low, high = (rows[LINE * k : LINE * k + STEPS, :] for k in (2 * part, 2 * part + 1))
+            out[part, place] = jnp.concatenate([low, high], axis=0).T[GHOST : GHOST + OWN, :]
 
 
 def unpack_body(recv, x, r):
@@ -539,7 +545,7 @@
 
 
 FIELD = (STEPS, 8, 128)
-SCRATCH = [vmem(*FIELD), vmem(*FIELD), vmem(STEPS + 2, 8, 128), vmem(STEPS + 2, 8, 128), vmem(STEPS + 2, 8, 128), vmem(1024, 128), vmem(1024, 128)]
+SCRATCH = [vmem(*FIELD), vmem(*FIELD), vmem(STEPS + 2, 8, 128), vmem(STEPS + 2, 8, 128), vmem(STEPS + 2, 8, 128), vmem(8 * SLAB, 128), vmem(8 * SLAB, 128)]
 
 
 def all_sums(gram):
@@ -609,7 +615,7 @@
             shape(HALF, *FIELD),
             shape(256, 128),
         ),
-        scratch_shapes=[vmem(7, 512, 128), vmem(7, STEPS + 2, 8, 128), *SCRATCH],
+        scratch_shapes=[vmem(7, 8 * LINE, 128), vmem(7, STEPS + 2, 8, 128), *SCRATCH],
         name="phase_one",
         compiler_params=params(),
     )(own, facing)
@@ -631,7 +637,7 @@
     pieces = pl.pallas_call(
         last_body,
         out_shape=shape(4, 2, OWN, 128),
-        scratch_shapes=[vmem(512, 128), vmem(512, 128)],
+        scratch_shapes=[vmem(8 * LINE, 128), vmem(8 * LINE, 128)],
         name="combine",
         compiler_params=params(),
     )(sums, y1, r4, v1, w1, v2, w2)

time: 147 us -> 146 us (level)
  no operation moved by 1% of the time
where the time goes in v6:
time: 146 us; the launch traced here: 145 us
  blocking collectives  62.6 us (43%)
  waiting for transfers between devices  31.6 us (22%)
  Pallas kernels  28.5 us (20%)
  starting transfers between devices  19.1 us (13%)
  local copies, waits for them, and re-layouts  2.13 us (1%)
    all_to_all x2, blocking collectives, all_sums(): lax.all_to_all(gram, ('lat', *LON), split_axis=0, concat_axis=0, tiled=True)  43 us
    ppermute x1, waiting for transfers between devices, branch(): lax.ppermute(b, LON, [(d, (2 * q - d) % 64) for d in range(64)])  20.2 us
    all_to_all x2, blocking collectives, swap_lat(): lax.all_to_all(pieces, 'lat', split_axis=0, concat_axis=0, tiled=True)  19.7 us
    pallas_call x1, Pallas kernels, shards(): pl.pallas_call(first_body, out_shape=(shape(9, *FIELD), shape(6, STEPS +...  11.9 us
    ppermute x1, starting transfers between devices, branch(): lax.ppermute(b, LON, [(d, (2 * q - d) % 64) for d in range(64)])  10.8 us
    pallas_call x1, Pallas kernels, shards(): pl.pallas_call(second_body, out_shape=(shape(*FIELD), shape(8, 128), shap...  8.94 us
    ppermute x4, waiting for transfers between devices, ring(): return lax.ppermute(block, LON, [(d, (d + step) % 64) for d in range(64)])  6.68 us
    all_to_all x1, waiting for transfers between devices, swap_lat(): lax.all_to_all(pieces, 'lat', split_axis=0, concat_axis=0, tiled=True)  4.72 us
  transfers between devices with their start and end apart: 6, of which 5 were waited for; matrix products, arithmetic and copies ran while one was open for 1% of the time, Pallas kernels for 0%

profile of v6, /device:TPU:1, one launch (start us, length us, event | category | flops | bytes accessed | tf_op | source)
XLA Modules:
  0.0 145.4 jit_solution(14622579131217966222)
XLA Ops:
  1.4 1.2 pack.1.packed
  2.6 31.0 %conditional.2 = (f32[7,128,128]{2,1,0:T(8,128)}) conditional(s32[]{:T(128)} %clamp.3, f32[7,128,128]{2,1,0:T(8,128)S(1)} %pack.1.packed, f32[7,128,128]{2,1,0:T(8,128)S(1)} %pack.1.packed, f32[7,128,128]{2,1,0:T(8,128)S(1)} %pack.1.packed, f32[7,128,128]{2,1,0:T(8,128)S(1)} %pack.1.packed, ...), branch_computations={%region_0.1_spmd, %region_1.2_spmd, %region_2.3_spmd, %region_3.4_... | conditional | bytes 1835056 | solution.py:563
  2.6 10.8 %collective-permute-start.24 = (f32[7,128,128]{2,1,0:T(8,128)S(1)}, f32[7,128,128]{2,1,0:T(8,128)}, u32[]{:S(2)}, u32[]{:S(2)}) collective-permute-start(f32[7,128,128]{2,1,0:T(8,128)S(1)} %param.24), channel_id=1, source_target_pairs={{0,48},{1,47},{2,46},{3,45},{4,44},{5,43},{6,42},{7,41},{8,40},{9,... | collective-permute-start | bytes 1376264 | tf_op jit(solution)/shard_map/cond/branch_24_fun/ppermute | solution.py:561
  13.4 20.2 %collective-permute-done.24 = f32[7,128,128]{2,1,0:T(8,128)} collective-permute-done((f32[7,128,128]{2,1,0:T(8,128)S(1)}, f32[7,128,128]{2,1,0:T(8,128)}, u32[]{:S(2)}, u32[]{:S(2)}) %collective-permute-start.24) | collective-permute-done | bytes 458784 | tf_op jit(solution)/shard_map/cond/branch_24_fun/ppermute | solution.py:561
  33.6 9.3 %conditional.3 = (f32[7,72,128]{2,1,0:T(8,128)}, f32[7,128,128]{2,1,0:T(8,128)S(1)}, f32[7,72,128]{2,1,0:T(8,128)}) conditional(s32[]{:T(128)} %convert_element_type.3, f32[7,128,128]{2,1,0:T(8,128)} %get-tuple-element.115, f32[7,128,128]{2,1,0:T(8,128)} %get-tuple-element.115), branch_computations={%region_32.33_spmd, %region_33.34_spmd} | conditional | bytes 4014184 | solution.py:573
  33.6 1.1 fusion.1
  34.7 2.4 %collective-permute-start.35 = (f32[7,72,128]{2,1,0:T(8,128)S(1)}, f32[7,72,128]{2,1,0:T(8,128)}, u32[]{:S(2)}, u32[]{:S(2)}) collective-permute-start(f32[7,72,128]{2,1,0:T(8,128)S(1)} %get-tuple-element.105), channel_id=1, source_target_pairs={{0,1},{1,2},{2,3},{3,4},{4,5},{5,6},{6,7},{7,8},{8,9},{9,10},{10,1... | collective-permute-start | bytes 774152 | tf_op jit(solution)/shard_map/cond/branch_1_fun/ppermute | solution.py:556
  37.1 1.0 copy.47
  38.1 2.3 %collective-permute-done.35 = f32[7,72,128]{2,1,0:T(8,128)} collective-permute-done((f32[7,72,128]{2,1,0:T(8,128)S(1)}, f32[7,72,128]{2,1,0:T(8,128)}, u32[]{:S(2)}, u32[]{:S(2)}) %collective-permute-start.35) | collective-permute-done | bytes 258080 | tf_op jit(solution)/shard_map/cond/branch_1_fun/ppermute | solution.py:556
  40.3 2.6 %collective-permute-done.34 = f32[7,72,128]{2,1,0:T(8,128)} collective-permute-done((f32[7,72,128]{2,1,0:T(8,128)S(1)}, f32[7,72,128]{2,1,0:T(8,128)}, u32[]{:S(2)}, u32[]{:S(2)}) %collective-permute-start.34) | collective-permute-done | bytes 258080 | tf_op jit(solution)/shard_map/cond/branch_1_fun/ppermute | solution.py:556
  42.9 2.9 %select.17 = f32[4,7,48,128]{3,2,1,0:T(8,128)} custom-call(s32[1]{0:T(128)} %bitcast.1.shift, f32[7,72,128]{2,1,0:T(8,128)} %get-tuple-element.86.low, f32[7,128,128]{2,1,0:T(8,128)S(1)} %get-tuple-element.87.main, f32[7,72,128]{2,1,0:T(8,128)} %get-tuple-element.88.high), custom_call_target="tpu_custom_call" | custom-call | tf_op jit(solution)/shard_map/select/pallas_call | solution.py:597
  45.8 4.2 %all-to-all-start.1 = ((f32[4,7,48,128]{3,2,1,0:T(8,128)}), f32[4,7,48,128]{3,2,1,0:T(8,128)S(1)}, u32[]{:S(2)}, u32[]{:S(2)}) async-start(f32[4,7,48,128]{3,2,1,0:T(8,128)} %select.17), calls=%async_computation.1 | async-start | bytes 1376256 | tf_op jit(solution)/shard_map/all_to_all | solution.py:577
  50.0 0.1 collective-permute-start.37
  50.1 1.7 %collective-permute-start.36 = (f32[7,8,128]{2,1,0:T(8,128)S(1)}, f32[7,8,128]{2,1,0:T(8,128)S(1)}, u32[]{:S(2)}, u32[]{:S(2)}) collective-permute-start(f32[7,8,128]{2,1,0:T(8,128)S(1)} %get-tuple-element.108), channel_id=1, source_target_pairs={{0,1},{1,2},{2,3},{3,4},{4,5},{5,6},{6,7},{7,8},{8,9},{9,10},{10,1... | collective-permute-start | bytes 86024 | tf_op jit(solution)/shard_map/ppermute | solution.py:556
  51.8 1.8 %collective-permute-done.37.after = f32[7,8,128]{2,1,0:T(8,128)S(1)} collective-permute-done((f32[7,8,128]{2,1,0:T(8,128)S(1)}, f32[7,8,128]{2,1,0:T(8,128)S(1)}, u32[]{:S(2)}, u32[]{:S(2)}) %collective-permute-start.37) | collective-permute-done | bytes 28704 | tf_op jit(solution)/shard_map/ppermute | solution.py:556
  53.7 4.7 %all-to-all-done.1.facing = f32[4,7,48,128]{3,2,1,0:T(8,128)S(1)} async-done(((f32[4,7,48,128]{3,2,1,0:T(8,128)}), f32[4,7,48,128]{3,2,1,0:T(8,128)S(1)}, u32[]{:S(2)}, u32[]{:S(2)}) %all-to-all-start.1) | async-done | bytes 688160 | tf_op jit(solution)/shard_map/all_to_all | solution.py:577
  58.4 11.8 %all_to_all.37.own = f32[4,7,48,128]{3,2,1,0:T(8,128)S(1)} all-to-all(f32[4,7,48,128]{3,2,1,0:T(8,128)S(1)} %window.1), channel_id=1, replica_groups=mesh['lat'=4,'x'=4,'z'=8,'core'=2] {'lat'}, dimensions={0} | all-to-all | bytes 1376256 | tf_op jit(solution)/shard_map/all_to_all | solution.py:577
  70.2 11.9 %phase_one.1 = (f32[9,64,8,128]{3,2,1,0:T(8,128)S(1)}, f32[6,72,8,128]{3,2,1,0:T(8,128)S(1)}, f32[16,8,128]{2,1,0:T(8,128)S(1)}, f32[16,8,128]{2,1,0:T(8,128)S(1...) custom-call(f32[4,7,48,128]{3,2,1,0:T(8,128)S(1)} %all_to_all.37.own, ...), custom_call_target="tpu_custom_call" | custom-call | tf_op jit(solution)/shard_map/phase_one/pallas_call | solution.py:605
  82.1 21.3 %all_to_all.38 = f32[256,1,128]{2,1,0:T(1,128)S(1)} all-to-all(f32[256,1,128]{2,1,0:T(1,128)S(1)} %bitcast.12), channel_id=1, replica_groups=mesh['lat'=4,'x'=4,'z'=8,'core'=2] {'lat','x','z','core'}, dimensions={0} | all-to-all | bytes 262144 | tf_op jit(solution)/shard_map/all_to_all | solution.py:552
  103.4 8.9 %phase_two.1 = (f32[64,8,128]{2,1,0:T(8,128)S(1)}, f32[8,128]{1,0:T(8,128)S(1)}, f32[4,64,8,128]{3,2,1,0:T(8,128)S(1)}, f32[4,64,8,128]{3,2,1,0:T(8,128)S(1)}, f32[512,128]{1,0:T(8,128)S(1)}) custom-call(f32[256,128]{1,0:T(8,128)S(1)} %bitcast.10, f32[9,64,8,128]{3,2,1,0:T(8,128)S(1)} %get-tuple-element.90.coef, ...), custom_call_target="tpu_custom_call" | custom-call | tf_op jit(solution)/shard_map/phase_two/pallas_call | solution.py:623
  112.4 21.6 %all_to_all.39 = f32[256,2,128]{2,1,0:T(2,128)S(1)} all-to-all(f32[256,2,128]{2,1,0:T(2,128)S(1)} %bitcast.11), channel_id=1, replica_groups=mesh['lat'=4,'x'=4,'z'=8,'core'=2] {'lat','x','z','core'}, dimensions={0} | all-to-all | bytes 524288 | tf_op jit(solution)/shard_map/all_to_all | solution.py:552
  134.0 1.9 %combine.1 = f32[4,2,32,128]{3,2,1,0:T(8,128)S(1)} custom-call(f32[512,128]{1,0:T(8,128)S(1)} %bitcast.9, f32[8,128]{1,0:T(8,128)S(1)} %get-tuple-element.99.y1, f32[64,8,128]{2,1,0:T(8,128)S(1)} %get-tuple-element.100.r_ref, f32[4,64,8,128]{3,2,1,0:T(8,128)S(1)} %get-tuple-element.96.v1, f32[4,64,8,128]{3,2,1,0:T(8,128)S(1)} %get-tuple-element.97.w1, ...), custom_call_target="tpu_custom_call" | custom-call | tf_op jit(solution)/shard_map/combine/pallas_call | solution.py:637
  135.9 7.9 %all_to_all.40.recv = f32[4,2,32,128]{3,2,1,0:T(8,128)} all-to-all(f32[4,2,32,128]{3,2,1,0:T(8,128)S(1)} %combine.1), channel_id=1, replica_groups=mesh['lat'=4,'x'=4,'z'=8,'core'=2] {'lat'}, dimensions={0} | all-to-all | bytes 262144 | tf_op jit(solution)/shard_map/all_to_all | solution.py:577
  143.8 1.7 %unpack.1 = (f32[128,128]{1,0:T(8,128)}, f32[128,128]{1,0:T(8,128)}) custom-call(f32[4,2,32,128]{3,2,1,0:T(8,128)} %all_to_all.40.recv), custom_call_target="tpu_custom_call" | custom-call | tf_op jit(solution)/shard_map/unpack/pallas_call | solution.py:645
  (4 shorter events, 0.1 us)
Async XLA Ops:
  2.6 30.9 %collective-permute-start.24 = (f32[7,128,128]{2,1,0:T(8,128)S(1)}, f32[7,128,128]{2,1,0:T(8,128)}, u32[]{:S(2)}, u32[]{:S(2)}) collective-permute-start(f32[7,128,128]{2,1,0:T(8,128)S(1)} %param.24), channel_id=1, source_target_pairs={{0,48},{1,47},{2,46},{3,45},{4,44},{5,43},{6,42},{7,41},{8,40},{9,... | collective-permute-start | bytes 1376264 | tf_op jit(solution)/shard_map/cond/branch_24_fun/ppermute | solution.py:561
  34.7 5.7 %collective-permute-start.35 = (f32[7,72,128]{2,1,0:T(8,128)S(1)}, f32[7,72,128]{2,1,0:T(8,128)}, u32[]{:S(2)}, u32[]{:S(2)}) collective-permute-start(f32[7,72,128]{2,1,0:T(8,128)S(1)} %get-tuple-element.105), channel_id=1, source_target_pairs={{0,1},{1,2},{2,3},{3,4},{4,5},{5,6},{6,7},{7,8},{8,9},{9,10},{10,1... | collective-permute-start | bytes 774152 | tf_op jit(solution)/shard_map/cond/branch_1_fun/ppermute | solution.py:556
  37.1 5.9 %collective-permute-start.34 = (f32[7,72,128]{2,1,0:T(8,128)S(1)}, f32[7,72,128]{2,1,0:T(8,128)}, u32[]{:S(2)}, u32[]{:S(2)}) collective-permute-start(f32[7,72,128]{2,1,0:T(8,128)S(1)} %get-tuple-element.106), channel_id=1, source_target_pairs={{0,63},{1,0},{2,1},{3,2},{4,3},{5,4},{6,5},{7,6},{8,7},{9,8},{10,9... | collective-permute-start | bytes 774152 | tf_op jit(solution)/shard_map/cond/branch_1_fun/ppermute | solution.py:556
  45.8 12.6 %all-to-all-start.1 = ((f32[4,7,48,128]{3,2,1,0:T(8,128)}), f32[4,7,48,128]{3,2,1,0:T(8,128)S(1)}, u32[]{:S(2)}, u32[]{:S(2)}) async-start(f32[4,7,48,128]{3,2,1,0:T(8,128)} %select.17), calls=%async_computation.1 | async-start | bytes 1376256 | tf_op jit(solution)/shard_map/all_to_all | solution.py:577
  50.0 3.7 %collective-permute-start.37 = (f32[7,8,128]{2,1,0:T(8,128)S(1)}, f32[7,8,128]{2,1,0:T(8,128)S(1)}, u32[]{:S(2)}, u32[]{:S(2)}) collective-permute-start(f32[7,8,128]{2,1,0:T(8,128)S(1)} %get-tuple-element.107), channel_id=1, source_target_pairs={{0,63},{1,0},{2,1},{3,2},{4,3},{5,4},{6,5},{7,6},{8,7},{9,8},{10,9... | collective-permute-start | bytes 86024 | tf_op jit(solution)/shard_map/ppermute | solution.py:556
  50.1 3.6 %collective-permute-start.36 = (f32[7,8,128]{2,1,0:T(8,128)S(1)}, f32[7,8,128]{2,1,0:T(8,128)S(1)}, u32[]{:S(2)}, u32[]{:S(2)}) collective-permute-start(f32[7,8,128]{2,1,0:T(8,128)S(1)} %get-tuple-element.108), channel_id=1, source_target_pairs={{0,1},{1,2},{2,3},{3,4},{4,5},{5,6},{6,7},{7,8},{8,9},{9,10},{10,1... | collective-permute-start | bytes 86024 | tf_op jit(solution)/shard_map/ppermute | solution.py:556

commit v7 on v6

--- a/solution.py
+++ b/solution.py
@@ -219,7 +219,7 @@
         finish(t0, g)
         return 0
 
-    lax.fori_loop(0, STEPS // 8, combine, 0, unroll=2)
+    lax.fori_loop(0, STEPS // 8, combine, 0, unroll=4)
 
 
 def operate(v_ref, place, w_ref, coef, fold, vp, ve, vw):
@@ -239,7 +239,7 @@
         w_ref[place, at] = out - (side + north + south)
         return 0
 
-    lax.fori_loop(0, STEPS // 4, step, 0, unroll=2)
+    lax.fori_loop(0, STEPS // 4, step, 0, unroll=4)
     w_ref[place, STEPS - 1] = w_ref[place, STEPS - 1] - fold[...] * facing_of(v_ref[place, STEPS - 1])
 
 
@@ -269,7 +269,7 @@
             packed[k, c] = out
         return 0
 
-    lax.fori_loop(0, STEPS // 4, step, 0)
+    lax.fori_loop(0, STEPS // 4, step, 0, unroll=2)
 
 
 def gram_row(lefts, rights, pairs, exact, columns, highs, lows, out):
@@ -378,7 +378,7 @@
         vw[t] = o * (surface + coef[N, t] + coef[S, t]) + (1.0 - o)
         return 0
 
-    lax.fori_loop(0, STEPS, weigh, 0, unroll=2)
+    lax.fori_loop(0, STEPS, weigh, 0, unroll=4)
     o = top_ocean
     coef[DIAG, STEPS - 1] = coef[DIAG, STEPS - 1] + o * fold_open
 

time: 146 us -> 143 us (0.979)
  Pallas kernels: 28.5 us -> 25.6 us
    pallas_call x1, Pallas kernels: 11.9 us -> 10.2 us  [shards(): pl.pallas_call(first_body, out_shape=(shape(9, *FIELD), shape(6, STEPS +...]
where the time goes in v7:
time: 143 us
  blocking collectives  62.6 us (44%)
  waiting for transfers between devices  31.6 us (22%)
  Pallas kernels  25.6 us (18%)
  starting transfers between devices  19.1 us (13%)
  local copies, waits for them, and re-layouts  2.13 us (1%)
    all_to_all x2, blocking collectives, all_sums(): lax.all_to_all(gram, ('lat', *LON), split_axis=0, concat_axis=0, tiled=True)  43 us
    ppermute x1, waiting for transfers between devices, branch(): lax.ppermute(b, LON, [(d, (2 * q - d) % 64) for d in range(64)])  20.2 us
    all_to_all x2, blocking collectives, swap_lat(): lax.all_to_all(pieces, 'lat', split_axis=0, concat_axis=0, tiled=True)  19.7 us
    ppermute x1, starting transfers between devices, branch(): lax.ppermute(b, LON, [(d, (2 * q - d) % 64) for d in range(64)])  10.8 us
    pallas_call x1, Pallas kernels, shards(): pl.pallas_call(first_body, out_shape=(shape(9, *FIELD), shape(6, STEPS +...  10.2 us
    pallas_call x1, Pallas kernels, shards(): pl.pallas_call(second_body, out_shape=(shape(*FIELD), shape(8, 128), shap...  7.72 us
    ppermute x4, waiting for transfers between devices, ring(): return lax.ppermute(block, LON, [(d, (d + step) % 64) for d in range(64)])  6.68 us
    all_to_all x1, waiting for transfers between devices, swap_lat(): lax.all_to_all(pieces, 'lat', split_axis=0, concat_axis=0, tiled=True)  4.72 us
  transfers between devices with their start and end apart: 6, of which 5 were waited for; matrix products, arithmetic and copies ran while one was open for 1% of the time, Pallas kernels for 0%

profile of v7, /device:TPU:1, one launch (start us, length us, event | category | flops | bytes accessed | tf_op | source)
XLA Modules:
  0.0 142.5 jit_solution(11627918195906256090)
XLA Ops:
  1.4 1.2 pack.1.packed
  2.6 31.0 %conditional.2 = (f32[7,128,128]{2,1,0:T(8,128)}) conditional(s32[]{:T(128)} %clamp.3, f32[7,128,128]{2,1,0:T(8,128)S(1)} %pack.1.packed, f32[7,128,128]{2,1,0:T(8,128)S(1)} %pack.1.packed, f32[7,128,128]{2,1,0:T(8,128)S(1)} %pack.1.packed, f32[7,128,128]{2,1,0:T(8,128)S(1)} %pack.1.packed, ...), branch_computations={%region_0.1_spmd, %region_1.2_spmd, %region_2.3_spmd, %region_3.4_... | conditional | bytes 1835056 | solution.py:563
  2.6 10.8 %collective-permute-start.24 = (f32[7,128,128]{2,1,0:T(8,128)S(1)}, f32[7,128,128]{2,1,0:T(8,128)}, u32[]{:S(2)}, u32[]{:S(2)}) collective-permute-start(f32[7,128,128]{2,1,0:T(8,128)S(1)} %param.24), channel_id=1, source_target_pairs={{0,48},{1,47},{2,46},{3,45},{4,44},{5,43},{6,42},{7,41},{8,40},{9,... | collective-permute-start | bytes 1376264 | tf_op jit(solution)/shard_map/cond/branch_24_fun/ppermute | solution.py:561
  13.4 20.2 %collective-permute-done.24 = f32[7,128,128]{2,1,0:T(8,128)} collective-permute-done((f32[7,128,128]{2,1,0:T(8,128)S(1)}, f32[7,128,128]{2,1,0:T(8,128)}, u32[]{:S(2)}, u32[]{:S(2)}) %collective-permute-start.24) | collective-permute-done | bytes 458784 | tf_op jit(solution)/shard_map/cond/branch_24_fun/ppermute | solution.py:561
  33.6 9.3 %conditional.3 = (f32[7,72,128]{2,1,0:T(8,128)}, f32[7,128,128]{2,1,0:T(8,128)S(1)}, f32[7,72,128]{2,1,0:T(8,128)}) conditional(s32[]{:T(128)} %convert_element_type.3, f32[7,128,128]{2,1,0:T(8,128)} %get-tuple-element.115, f32[7,128,128]{2,1,0:T(8,128)} %get-tuple-element.115), branch_computations={%region_32.33_spmd, %region_33.34_spmd} | conditional | bytes 4014184 | solution.py:573
  33.6 1.1 fusion.1
  34.7 2.4 %collective-permute-start.35 = (f32[7,72,128]{2,1,0:T(8,128)S(1)}, f32[7,72,128]{2,1,0:T(8,128)}, u32[]{:S(2)}, u32[]{:S(2)}) collective-permute-start(f32[7,72,128]{2,1,0:T(8,128)S(1)} %get-tuple-element.105), channel_id=1, source_target_pairs={{0,1},{1,2},{2,3},{3,4},{4,5},{5,6},{6,7},{7,8},{8,9},{9,10},{10,1... | collective-permute-start | bytes 774152 | tf_op jit(solution)/shard_map/cond/branch_1_fun/ppermute | solution.py:556
  37.1 1.0 copy.47
  38.1 2.3 %collective-permute-done.35 = f32[7,72,128]{2,1,0:T(8,128)} collective-permute-done((f32[7,72,128]{2,1,0:T(8,128)S(1)}, f32[7,72,128]{2,1,0:T(8,128)}, u32[]{:S(2)}, u32[]{:S(2)}) %collective-permute-start.35) | collective-permute-done | bytes 258080 | tf_op jit(solution)/shard_map/cond/branch_1_fun/ppermute | solution.py:556
  40.3 2.6 %collective-permute-done.34 = f32[7,72,128]{2,1,0:T(8,128)} collective-permute-done((f32[7,72,128]{2,1,0:T(8,128)S(1)}, f32[7,72,128]{2,1,0:T(8,128)}, u32[]{:S(2)}, u32[]{:S(2)}) %collective-permute-start.34) | collective-permute-done | bytes 258080 | tf_op jit(solution)/shard_map/cond/branch_1_fun/ppermute | solution.py:556
  42.9 2.9 %select.17 = f32[4,7,48,128]{3,2,1,0:T(8,128)} custom-call(s32[1]{0:T(128)} %bitcast.1.shift, f32[7,72,128]{2,1,0:T(8,128)} %get-tuple-element.86.low, f32[7,128,128]{2,1,0:T(8,128)S(1)} %get-tuple-element.87.main, f32[7,72,128]{2,1,0:T(8,128)} %get-tuple-element.88.high), custom_call_target="tpu_custom_call" | custom-call | tf_op jit(solution)/shard_map/select/pallas_call | solution.py:597
  45.8 4.2 %all-to-all-start.1 = ((f32[4,7,48,128]{3,2,1,0:T(8,128)}), f32[4,7,48,128]{3,2,1,0:T(8,128)S(1)}, u32[]{:S(2)}, u32[]{:S(2)}) async-start(f32[4,7,48,128]{3,2,1,0:T(8,128)} %select.17), calls=%async_computation.1 | async-start | bytes 1376256 | tf_op jit(solution)/shard_map/all_to_all | solution.py:577
  50.0 0.1 collective-permute-start.37
  50.1 1.7 %collective-permute-start.36 = (f32[7,8,128]{2,1,0:T(8,128)S(1)}, f32[7,8,128]{2,1,0:T(8,128)S(1)}, u32[]{:S(2)}, u32[]{:S(2)}) collective-permute-start(f32[7,8,128]{2,1,0:T(8,128)S(1)} %get-tuple-element.108), channel_id=1, source_target_pairs={{0,1},{1,2},{2,3},{3,4},{4,5},{5,6},{6,7},{7,8},{8,9},{9,10},{10,1... | collective-permute-start | bytes 86024 | tf_op jit(solution)/shard_map/ppermute | solution.py:556
  51.8 1.8 %collective-permute-done.37.after = f32[7,8,128]{2,1,0:T(8,128)S(1)} collective-permute-done((f32[7,8,128]{2,1,0:T(8,128)S(1)}, f32[7,8,128]{2,1,0:T(8,128)S(1)}, u32[]{:S(2)}, u32[]{:S(2)}) %collective-permute-start.37) | collective-permute-done | bytes 28704 | tf_op jit(solution)/shard_map/ppermute | solution.py:556
  53.7 4.7 %all-to-all-done.1.facing = f32[4,7,48,128]{3,2,1,0:T(8,128)S(1)} async-done(((f32[4,7,48,128]{3,2,1,0:T(8,128)}), f32[4,7,48,128]{3,2,1,0:T(8,128)S(1)}, u32[]{:S(2)}, u32[]{:S(2)}) %all-to-all-start.1) | async-done | bytes 688160 | tf_op jit(solution)/shard_map/all_to_all | solution.py:577
  58.4 11.8 %all_to_all.37.own = f32[4,7,48,128]{3,2,1,0:T(8,128)S(1)} all-to-all(f32[4,7,48,128]{3,2,1,0:T(8,128)S(1)} %window.1), channel_id=1, replica_groups=mesh['lat'=4,'x'=4,'z'=8,'core'=2] {'lat'}, dimensions={0} | all-to-all | bytes 1376256 | tf_op jit(solution)/shard_map/all_to_all | solution.py:577
  70.2 10.2 %phase_one.1 = (f32[9,64,8,128]{3,2,1,0:T(8,128)S(1)}, f32[6,72,8,128]{3,2,1,0:T(8,128)S(1)}, f32[16,8,128]{2,1,0:T(8,128)S(1)}, f32[16,8,128]{2,1,0:T(8,128)S(1...) custom-call(f32[4,7,48,128]{3,2,1,0:T(8,128)S(1)} %all_to_all.37.own, ...), custom_call_target="tpu_custom_call" | custom-call | tf_op jit(solution)/shard_map/phase_one/pallas_call | solution.py:605
  80.4 21.3 %all_to_all.38 = f32[256,1,128]{2,1,0:T(1,128)S(1)} all-to-all(f32[256,1,128]{2,1,0:T(1,128)S(1)} %bitcast.12), channel_id=1, replica_groups=mesh['lat'=4,'x'=4,'z'=8,'core'=2] {'lat','x','z','core'}, dimensions={0} | all-to-all | bytes 262144 | tf_op jit(solution)/shard_map/all_to_all | solution.py:552
  101.7 7.7 %phase_two.1 = (f32[64,8,128]{2,1,0:T(8,128)S(1)}, f32[8,128]{1,0:T(8,128)S(1)}, f32[4,64,8,128]{3,2,1,0:T(8,128)S(1)}, f32[4,64,8,128]{3,2,1,0:T(8,128)S(1)}, f32[512,128]{1,0:T(8,128)S(1)}) custom-call(f32[256,128]{1,0:T(8,128)S(1)} %bitcast.10, f32[9,64,8,128]{3,2,1,0:T(8,128)S(1)} %get-tuple-element.90.coef, ...), custom_call_target="tpu_custom_call" | custom-call | tf_op jit(solution)/shard_map/phase_two/pallas_call | solution.py:623
  109.4 21.6 %all_to_all.39 = f32[256,2,128]{2,1,0:T(2,128)S(1)} all-to-all(f32[256,2,128]{2,1,0:T(2,128)S(1)} %bitcast.11), channel_id=1, replica_groups=mesh['lat'=4,'x'=4,'z'=8,'core'=2] {'lat','x','z','core'}, dimensions={0} | all-to-all | bytes 524288 | tf_op jit(solution)/shard_map/all_to_all | solution.py:552
  131.1 1.9 %combine.1 = f32[4,2,32,128]{3,2,1,0:T(8,128)S(1)} custom-call(f32[512,128]{1,0:T(8,128)S(1)} %bitcast.9, f32[8,128]{1,0:T(8,128)S(1)} %get-tuple-element.99.y1, f32[64,8,128]{2,1,0:T(8,128)S(1)} %get-tuple-element.100.r_ref, f32[4,64,8,128]{3,2,1,0:T(8,128)S(1)} %get-tuple-element.96.v1, f32[4,64,8,128]{3,2,1,0:T(8,128)S(1)} %get-tuple-element.97.w1, ...), custom_call_target="tpu_custom_call" | custom-call | tf_op jit(solution)/shard_map/combine/pallas_call | solution.py:637
  133.0 7.9 %all_to_all.40.recv = f32[4,2,32,128]{3,2,1,0:T(8,128)} all-to-all(f32[4,2,32,128]{3,2,1,0:T(8,128)S(1)} %combine.1), channel_id=1, replica_groups=mesh['lat'=4,'x'=4,'z'=8,'core'=2] {'lat'}, dimensions={0} | all-to-all | bytes 262144 | tf_op jit(solution)/shard_map/all_to_all | solution.py:577
  140.9 1.7 %unpack.1 = (f32[128,128]{1,0:T(8,128)}, f32[128,128]{1,0:T(8,128)}) custom-call(f32[4,2,32,128]{3,2,1,0:T(8,128)} %all_to_all.40.recv), custom_call_target="tpu_custom_call" | custom-call | tf_op jit(solution)/shard_map/unpack/pallas_call | solution.py:645
  (4 shorter events, 0.1 us)
Async XLA Ops:
  2.6 30.9 %collective-permute-start.24 = (f32[7,128,128]{2,1,0:T(8,128)S(1)}, f32[7,128,128]{2,1,0:T(8,128)}, u32[]{:S(2)}, u32[]{:S(2)}) collective-permute-start(f32[7,128,128]{2,1,0:T(8,128)S(1)} %param.24), channel_id=1, source_target_pairs={{0,48},{1,47},{2,46},{3,45},{4,44},{5,43},{6,42},{7,41},{8,40},{9,... | collective-permute-start | bytes 1376264 | tf_op jit(solution)/shard_map/cond/branch_24_fun/ppermute | solution.py:561
  34.7 5.7 %collective-permute-start.35 = (f32[7,72,128]{2,1,0:T(8,128)S(1)}, f32[7,72,128]{2,1,0:T(8,128)}, u32[]{:S(2)}, u32[]{:S(2)}) collective-permute-start(f32[7,72,128]{2,1,0:T(8,128)S(1)} %get-tuple-element.105), channel_id=1, source_target_pairs={{0,1},{1,2},{2,3},{3,4},{4,5},{5,6},{6,7},{7,8},{8,9},{9,10},{10,1... | collective-permute-start | bytes 774152 | tf_op jit(solution)/shard_map/cond/branch_1_fun/ppermute | solution.py:556
  37.1 5.9 %collective-permute-start.34 = (f32[7,72,128]{2,1,0:T(8,128)S(1)}, f32[7,72,128]{2,1,0:T(8,128)}, u32[]{:S(2)}, u32[]{:S(2)}) collective-permute-start(f32[7,72,128]{2,1,0:T(8,128)S(1)} %get-tuple-element.106), channel_id=1, source_target_pairs={{0,63},{1,0},{2,1},{3,2},{4,3},{5,4},{6,5},{7,6},{8,7},{9,8},{10,9... | collective-permute-start | bytes 774152 | tf_op jit(solution)/shard_map/cond/branch_1_fun/ppermute | solution.py:556
  45.8 12.6 %all-to-all-start.1 = ((f32[4,7,48,128]{3,2,1,0:T(8,128)}), f32[4,7,48,128]{3,2,1,0:T(8,128)S(1)}, u32[]{:S(2)}, u32[]{:S(2)}) async-start(f32[4,7,48,128]{3,2,1,0:T(8,128)} %select.17), calls=%async_computation.1 | async-start | bytes 1376256 | tf_op jit(solution)/shard_map/all_to_all | solution.py:577
  50.0 3.7 %collective-permute-start.37 = (f32[7,8,128]{2,1,0:T(8,128)S(1)}, f32[7,8,128]{2,1,0:T(8,128)S(1)}, u32[]{:S(2)}, u32[]{:S(2)}) collective-permute-start(f32[7,8,128]{2,1,0:T(8,128)S(1)} %get-tuple-element.107), channel_id=1, source_target_pairs={{0,63},{1,0},{2,1},{3,2},{4,3},{5,4},{6,5},{7,6},{8,7},{9,8},{10,9... | collective-permute-start | bytes 86024 | tf_op jit(solution)/shard_map/ppermute | solution.py:556
  50.1 3.6 %collective-permute-start.36 = (f32[7,8,128]{2,1,0:T(8,128)S(1)}, f32[7,8,128]{2,1,0:T(8,128)S(1)}, u32[]{:S(2)}, u32[]{:S(2)}) collective-permute-start(f32[7,8,128]{2,1,0:T(8,128)S(1)} %get-tuple-element.108), channel_id=1, source_target_pairs={{0,1},{1,2},{2,3},{3,4},{4,5},{5,6},{6,7},{7,8},{8,9},{9,10},{10,1... | collective-permute-start | bytes 86024 | tf_op jit(solution)/shard_map/ppermute | solution.py:556
